TPU v7x, 32 devices: a whole 2x2x4 slice. The times are simulated.
32 devices in a mesh: ep: 8 (over z, y), rep: 4 (over x, core).
Axes of the slice: x: 2, y: 2, z: 4, core: 2. Of those that a mesh axis runs over, the one named last changes fastest.
Arguments:
- tokens: bfloat16 [4096, 2304], P(('ep', 'rep')), may hold values from -6 to 6
- output_grad: bfloat16 [4096, 2304], P(('ep', 'rep')), may hold values from -2 to 2
- chosen_experts: int32 [4096, 8], P(('ep', 'rep')), may hold values from 0 to 31, all different within a row; in each aligned block of 128 rows (0 to 127, 128 to 255, ...) at most 36 rows name the same one
- route_weights: float32 [4096, 8], P(('ep', 'rep')), may hold values from 0.1 to 0.5
- gate_weight: bfloat16 [32, 2304, 1024], P(('ep', 'rep')), may hold values from -0.125 to 0.125
- up_weight: bfloat16 [32, 2304, 1024], P(('ep', 'rep')), may hold values from -0.125 to 0.125
- down_weight: bfloat16 [32, 1024, 2304], P(('ep', 'rep')), may hold values from -0.1875 to 0.1875
- gate_adapter_in: bfloat16 [32, 16, 2304], P(('ep', 'rep')), may hold values from -0.125 to 0.125
- gate_adapter_out: bfloat16 [32, 16, 1024], P(('ep', 'rep')), may hold values from -1 to 1
- up_adapter_in: bfloat16 [32, 16, 2304], P(('ep', 'rep')), may hold values from -0.125 to 0.125
- up_adapter_out: bfloat16 [32, 16, 1024], P(('ep', 'rep')), may hold values from -1 to 1
- shared_gate: bfloat16 [2304, 512], P(None, 'rep'), may hold values from -0.125 to 0.125
- shared_up: bfloat16 [2304, 512], P(None, 'rep'), may hold values from -0.125 to 0.125
- shared_down: bfloat16 [2304, 512], P(None, 'rep'), may hold values from -0.25 to 0.25
Outputs:
- token_grad: bfloat16 [4096, 2304], P(('ep', 'rep'))
- gate_in_grad: float32 [32, 16, 2304], P(('ep', 'rep'))
- gate_out_grad: float32 [32, 16, 1024], P(('ep', 'rep'))
- up_in_grad: float32 [32, 16, 2304], P(('ep', 'rep'))
- up_out_grad: float32 [32, 16, 1024], P(('ep', 'rep'))
Inputs may be any that keep to these rules, and one draw needn't show every extreme that they name: `chosen_experts`: each row names 8 different experts. In each aligned block of 128 rows no expert is named by more than 36 rows, and in some block an expert is named by exactly 36 rows.
All inputs are finite; a program needn't handle non-finite values.
Results may differ from a plain program's by a relative error of at most 0.0064.
Values may be sent and summed in bfloat16 or wider, within the bound.
No kernel may reach another device: no remote copies, remote signals or barrier semaphores. Data moves between devices by JAX's collectives and lax.ppermute only.
A program may use at most 128 MiB of HBM per device.

v0:
```python
import functools

import jax
import jax.numpy as jnp
from jax import lax
from jax.experimental import pallas as pl
from jax.experimental.pallas import tpu as pltpu
from jax.sharding import PartitionSpec as P


AXES = ("ep", "rep")
F32 = jnp.float32
BF16 = jnp.bfloat16


def dot(left, right, left_dim, right_dim):
    return lax.dot_general(
        left, right, (((left_dim,), (right_dim,)), ((), ())), preferred_element_type=F32
    )


def cotangents(gate_pre, up_pre, d_hidden):
    sig = jax.nn.sigmoid(gate_pre)
    d_gate = (d_hidden * up_pre * sig * (1.0 + gate_pre * (1.0 - sig))).astype(BF16)
    d_up = (d_hidden * gate_pre * sig).astype(BF16)
    return d_gate, d_up


def params(mib=56):
    return pltpu.CompilerParams(vmem_limit_bytes=mib * 1024 * 1024)


def selection(info_refs, peers, cap, want_weights):
    count = len(info_refs)
    info = [ref[...] for ref in info_refs]
    tokens = info[0].shape[1]
    places = jnp.concatenate(
        [jnp.where(a[:peers] >= 0.0, a[:peers] + float(i * cap), -1.0) for i, a in enumerate(info)],
        axis=1,
    )
    row = lax.broadcasted_iota(jnp.int32, (count * cap, count * tokens), 0).astype(F32)
    hot = [(row == places[d : d + 1, :]).astype(F32) for d in range(peers)]
    scale = None
    if want_weights:
        weights = jnp.concatenate([a[peers : 2 * peers] for a in info], axis=1)
        scale = jnp.concatenate(
            [
                jnp.sum(hot[d] * weights[d : d + 1, :], axis=1, keepdims=True)
                for d in range(peers)
            ],
            axis=0,
        )
    return jnp.concatenate(hot, axis=0), scale


def pack_kernel(peers, cap, count, scaled, *refs):
    info_refs, block_refs, out_refs = refs[:count], refs[count : 2 * count], refs[2 * count :]
    hot, scale = selection(info_refs, peers, cap, scaled)
    rows = jnp.concatenate([ref[...] for ref in block_refs], axis=0)
    picked = dot(hot.astype(BF16), rows, 1, 0)
    if scaled:
        picked = picked * scale
    for d in range(peers):
        out_refs[d][...] = picked[d * count * cap : (d + 1) * count * cap].astype(BF16)


def pack(infos, blocks, peers, cap, scaled):
    count = len(infos)
    tokens, width = blocks[0].shape
    tile = width // 3 if width % 384 == 0 else width
    whole = pl.BlockSpec(infos[0].shape, lambda i: (0, 0))
    part = pl.BlockSpec((tokens, tile), lambda i: (0, i))
    return pl.pallas_call(
        functools.partial(pack_kernel, peers, cap, count, scaled),
        grid=(width // tile,),
        in_specs=[whole] * count + [part] * count,
        out_specs=[pl.BlockSpec((count * cap, tile), lambda i: (0, i))] * peers,
        out_shape=[jax.ShapeDtypeStruct((count * cap, width), BF16)] * peers,
        compiler_params=params(),
        cost_estimate=pl.CostEstimate(
            flops=2 * peers * count * cap * count * tokens * width,
            bytes_accessed=2 * width * (peers * count * cap + count * tokens),
            transcendentals=0,
        ),
    )(*infos, *blocks)


def merge_kernel(peers, cap, count, *refs):
    info_refs, back_refs, out_refs = refs[:count], refs[count : count + peers], refs[count + peers :]
    tokens = info_refs[0].shape[1]
    hot, _ = selection(info_refs, peers, cap, False)
    spread = jnp.transpose(hot).astype(BF16)
    back = jnp.concatenate([ref[...].astype(F32) for ref in back_refs], axis=0).astype(BF16)
    total = dot(spread, back, 1, 0)
    for i in range(count):
        out_refs[i][...] = total[i * tokens : (i + 1) * tokens].astype(out_refs[i].dtype)


def merge(infos, back, peers, cap, kinds):
    count = len(infos)
    tokens = infos[0].shape[1]
    width = back[0].shape[1]
    tile = width // 3 if width % 384 == 0 else width
    whole = pl.BlockSpec(infos[0].shape, lambda i: (0, 0))
    return pl.pallas_call(
        functools.partial(merge_kernel, peers, cap, count),
        grid=(width // tile,),
        in_specs=[whole] * count + [pl.BlockSpec((count * cap, tile), lambda i: (0, i))] * peers,
        out_specs=[pl.BlockSpec((tokens, tile), lambda i: (0, i))] * count,
        out_shape=[jax.ShapeDtypeStruct((tokens, width), kind) for kind in kinds],
        compiler_params=params(),
        cost_estimate=pl.CostEstimate(
            flops=2 * peers * count * cap * count * tokens * width,
            bytes_accessed=2 * width * (peers * count * cap + count * tokens),
            transcendentals=0,
        ),
    )(*infos, *back)


def expert_kernel(peers, steps, *refs):
    row_refs, grad_refs = refs[:peers], refs[peers : 2 * peers]
    gate_w, up_w, down_w, gate_in, gate_out, up_in, up_out = refs[2 * peers : 2 * peers + 7]
    out_refs = refs[2 * peers + 7 : 3 * peers + 7]
    gate_in_grad, gate_out_grad, up_in_grad, up_out_grad = refs[3 * peers + 7 : 3 * peers + 11]
    rows, grads, total, low_gate, low_up, back_gate, back_up = refs[3 * peers + 11 :]
    step = pl.program_id(0)
    height = row_refs[0].shape[0]

    @pl.when(step == 0)
    def _():
        rows[...] = jnp.concatenate([r[...].astype(F32) for r in row_refs], axis=0).astype(BF16)
        grads[...] = jnp.concatenate([r[...].astype(F32) for r in grad_refs], axis=0).astype(BF16)
        low_gate[...] = dot(rows[...], gate_in[...], 1, 1).astype(BF16)
        low_up[...] = dot(rows[...], up_in[...], 1, 1).astype(BF16)
        back_gate[...] = jnp.zeros_like(back_gate)
        back_up[...] = jnp.zeros_like(back_up)

    gate_pre = dot(rows[...], gate_w[...], 1, 0) + dot(low_gate[...], gate_out[...], 1, 0)
    up_pre = dot(rows[...], up_w[...], 1, 0) + dot(low_up[...], up_out[...], 1, 0)
    d_hidden = dot(grads[...], down_w[...], 1, 1)
    d_gate, d_up = cotangents(gate_pre, up_pre, d_hidden)
    back_gate[...] += dot(d_gate, gate_out[...], 1, 1)
    back_up[...] += dot(d_up, up_out[...], 1, 1)
    gate_out_grad[...] = dot(low_gate[...], d_gate, 0, 0)
    up_out_grad[...] = dot(low_up[...], d_up, 0, 0)
    part = dot(d_gate, gate_w[...], 1, 1) + dot(d_up, up_w[...], 1, 1)

    @pl.when(step == 0)
    def _():
        total[...] = part

    @pl.when(step > 0)
    def _():
        total[...] += part

    @pl.when(step == steps - 1)
    def _():
        low_dgate = back_gate[...].astype(BF16)
        low_dup = back_up[...].astype(BF16)
        done = total[...] + dot(low_dgate, gate_in[...], 1, 0) + dot(low_dup, up_in[...], 1, 0)
        for d in range(peers):
            out_refs[d][...] = done[d * height : (d + 1) * height].astype(BF16)
        gate_in_grad[...] = dot(low_dgate, rows[...], 0, 0)
        up_in_grad[...] = dot(low_dup, rows[...], 0, 0)


def expert(rows, grads, weights):
    peers = len(rows)
    height, width = rows[0].shape
    gate_w, _, _, gate_in, _, _, _ = weights
    hidden = gate_w.shape[1]
    rank = gate_in.shape[0]
    tile = 256 if hidden % 256 == 0 else hidden
    steps = hidden // tile
    count = peers * height
    block = pl.BlockSpec((height, width), lambda i: (0, 0))
    wide = pl.BlockSpec((width, tile), lambda i: (0, i))
    low_in = pl.BlockSpec((rank, width), lambda i: (0, 0))
    low_out = pl.BlockSpec((rank, tile), lambda i: (0, i))
    return pl.pallas_call(
        functools.partial(expert_kernel, peers, steps),
        grid=(steps,),
        in_specs=[block] * (2 * peers)
        + [wide, wide, pl.BlockSpec((tile, width), lambda i: (i, 0)), low_in, low_out, low_in, low_out],
        out_specs=[block] * peers + [low_in, low_out, low_in, low_out],
        out_shape=[jax.ShapeDtypeStruct((height, width), BF16)] * peers
        + [
            jax.ShapeDtypeStruct((rank, width), F32),
            jax.ShapeDtypeStruct((rank, hidden), F32),
            jax.ShapeDtypeStruct((rank, width), F32),
            jax.ShapeDtypeStruct((rank, hidden), F32),
        ],
        scratch_shapes=[
            pltpu.VMEM((count, width), BF16),
            pltpu.VMEM((count, width), BF16),
            pltpu.VMEM((count, width), F32),
            pltpu.VMEM((count, rank), BF16),
            pltpu.VMEM((count, rank), BF16),
            pltpu.VMEM((count, rank), F32),
            pltpu.VMEM((count, rank), F32),
        ],
        compiler_params=params(60),
        cost_estimate=pl.CostEstimate(
            flops=10 * count * width * hidden,
            bytes_accessed=6 * width * (count + hidden),
            transcendentals=count * hidden,
        ),
    )(*rows, *grads, *weights)


def shared_kernel(slices, *refs):
    rows, grads = refs[0], refs[1]
    gates, ups, downs = (refs[2 + i * slices : 2 + (i + 1) * slices] for i in range(3))
    out = refs[2 + 3 * slices]
    for i in range(slices):
        gate_w, up_w = gates[i][...], ups[i][...]
        gate_pre = dot(rows[...], gate_w, 1, 0)
        up_pre = dot(rows[...], up_w, 1, 0)
        d_hidden = dot(grads[...], downs[i][...], 1, 0)
        d_gate, d_up = cotangents(gate_pre, up_pre, d_hidden)
        part = dot(d_gate, gate_w, 1, 1) + dot(d_up, up_w, 1, 1)
        if i == 0:
            out[...] = part
        else:
            out[...] += part


def shared(rows, grads, gates, ups, downs):
    slices = len(gates)
    hidden = gates[0].shape[1]
    count, width = rows.shape
    return pl.pallas_call(
        functools.partial(shared_kernel, slices),
        out_shape=jax.ShapeDtypeStruct((count, width), F32),
        compiler_params=params(),
        cost_estimate=pl.CostEstimate(
            flops=10 * count * width * hidden * slices,
            bytes_accessed=6 * width * hidden * slices,
            transcendentals=count * hidden * slices,
        ),
        name="shared",
    )(rows, grads, *gates, *ups, *downs)


def halvings(count):
    bits = []
    while count > 1:
        count //= 2
        bits.append(count)
    return bits


def plane_groups(planes):
    return [list(range(0, planes, 2)), list(range(1, planes, 2))]


def local(
    tokens,
    output_grad,
    chosen_experts,
    route_weights,
    gate_weight,
    up_weight,
    down_weight,
    gate_adapter_in,
    gate_adapter_out,
    up_adapter_in,
    up_adapter_out,
    shared_gate,
    shared_up,
    shared_down,
):
    rep_count = lax.axis_size("rep")
    owners = lax.axis_size("ep") * rep_count
    peers = 2 * rep_count
    planes = owners // peers
    token_rows, _ = tokens.shape
    pick_count = chosen_experts.shape[1]
    cap = token_rows * pick_count * 9 // (8 * owners)
    me = lax.axis_index(AXES)

    def swap(array, plane_step, peer_step):
        step = plane_step * peers + peer_step
        if step == 0:
            return array
        return lax.ppermute(array, AXES, [(i, i ^ step) for i in range(owners)])

    ids = me ^ lax.broadcasted_iota(jnp.int32, (owners, 1, 1), 0)
    named = chosen_experts.T[None] == ids
    weight = jnp.sum(jnp.where(named, route_weights.T[None], 0.0), axis=1)
    picked = jnp.any(named, axis=1)
    earlier = (
        lax.broadcasted_iota(jnp.int32, (token_rows, token_rows), 0)
        < lax.broadcasted_iota(jnp.int32, (token_rows, token_rows), 1)
    ).astype(BF16)
    ahead = jnp.dot(picked.astype(BF16), earlier, preferred_element_type=F32)
    place = jnp.where(picked, ahead, -1.0)
    info = jnp.concatenate(
        [place.reshape(planes, peers, token_rows), weight.reshape(planes, peers, token_rows)], axis=1
    )

    groups = plane_groups(planes)
    infos = {p: swap(info[p], p, 0) for p in range(planes)}
    token_blocks, grad_blocks = {}, {}
    for group in groups:
        for p in group:
            token_blocks[p] = swap(tokens, p, 0)
        for p in group:
            grad_blocks[p] = swap(output_grad, p, 0)

    weights = (
        gate_weight[0],
        up_weight[0],
        down_weight[0],
        gate_adapter_in[0],
        gate_adapter_out[0],
        up_adapter_in[0],
        up_adapter_out[0],
    )
    slices = {"gate": [shared_gate], "up": [shared_up], "down": [shared_down]}
    for bit in halvings(rep_count):
        for kind, held in slices.items():
            slices[kind] = held + [swap(piece, 0, bit) for piece in held]

    parts = {}
    adapter = []
    for group in groups:
        seen = [infos[p] for p in group]
        row_out = pack(seen, [token_blocks[p] for p in group], peers, cap, False)
        grad_out = pack(seen, [grad_blocks[p] for p in group], peers, cap, True)
        rows = [swap(row_out[d], 0, d) for d in range(peers)]
        grads = [swap(grad_out[d], 0, d) for d in range(peers)]
        result = expert(rows, grads, weights)
        adapter.append(result[peers:])
        back = [swap(result[d], 0, d) for d in range(peers)]
        kinds = [F32 if p == 0 else BF16 for p in group]
        merged = merge(seen, back, peers, cap, kinds)
        for p, part in zip(group, merged):
            parts[p] = swap(part, p, 0)
    total = shared(tokens, output_grad, *slices.values())
    for p in range(planes):
        total = total + parts[p].astype(F32)
    token_grad = total.astype(BF16)
    adapter_grads = [sum(pieces[1:], pieces[0])[None] for pieces in zip(*adapter)]
    return (token_grad, *adapter_grads)


def solution(mesh):
    row = P(AXES, None)
    block = P(AXES, None, None)
    in_specs = (row,) * 4 + (block,) * 7 + (P(None, "rep"),) * 3
    out_specs = (row,) + (block,) * 4

    return jax.shard_map(local, mesh=mesh, in_specs=in_specs, out_specs=out_specs, check_vma=False)
```

profile of v0, /device:TPU:0, one launch (start us, length us, event | category | flops | bytes accessed | tf_op | source)
XLA Modules:
  0.0 412.6 jit_solution(4338077423716368161)
XLA Ops:
  0.6 3.1 collective-permute-start.35
  3.7 2.5 collective-permute-start.36
  12.1 17.5 %collective-permute-done.33.refs_0_ = f32[16,128]{1,0:T(8,128)S(1)} collective-permute-done((f32[16,128]{1,0:T(8,128)S(1)}, f32[16,128]{1,0:T(8,128)S(1)}, u32[]{:S(2)}, u32[]{:S(2)}) %collective-permute-start.33) | collective-permute-done | bytes 8224 | tf_op jit(solution)/shard_map/ppermute | solution.py:286
  29.6 2.5 collective-permute-start.44
  34.9 2.6 collective-permute-start.18
  39.0 4.1 shard_map.177
  43.1 5.0 %collective-permute-done.44.refs_2_ = bf16[128,2304]{1,0:T(8,128)(2,1)S(1)} collective-permute-done((bf16[128,2304]{1,0:T(8,128)(2,1)}, bf16[128,2304]{1,0:T(8,128)(2,1)S(1)}, u32[]{:S(2)}, u32[]{:S(2)}) %collective-permute-start.44) | collective-permute-done | bytes 589856 | tf_op jit(solution)/shard_map/ppermute | solution.py:286
  48.0 13.6 %collective-permute-done.45.refs_3_ = bf16[128,2304]{1,0:T(8,128)(2,1)S(1)} collective-permute-done((bf16[128,2304]{1,0:T(8,128)(2,1)}, bf16[128,2304]{1,0:T(8,128)(2,1)S(1)}, u32[]{:S(2)}, u32[]{:S(2)}) %collective-permute-start.45) | collective-permute-done | bytes 589856 | tf_op jit(solution)/shard_map/ppermute | solution.py:286
  63.2 36.7 %collective-permute-done.10.refs_3_ = bf16[128,2304]{1,0:T(8,128)(2,1)S(1)} collective-permute-done((bf16[128,2304]{1,0:T(8,128)(2,1)}, bf16[128,2304]{1,0:T(8,128)(2,1)S(1)}, u32[]{:S(2)}, u32[]{:S(2)}) %collective-permute-start.10) | collective-permute-done | bytes 589856 | tf_op jit(solution)/shard_map/ppermute | solution.py:286
  100.0 4.4 %shard_map.178 = (bf16[72,2304]{1,0:T(8,128)(2,1)}, bf16[72,2304]{1,0:T(8,128)(2,1)}, bf16[72,2304]{1,0:T(8,128)(2,1)}, bf16[72,2304]{1,0:T(8,128)(2,1)}, bf16[7...) custom-call(f32[16,128]{1,0:T(8,128)} %copy-done.30, ...), custom_call_target="tpu_custom_call" | custom-call | flops 679477248 | bytes 3833856 | tf_op jit(solution)/shard_map/pallas_call | solution.py:73
  104.3 5.6 %collective-permute-done.18.refs_3_ = bf16[128,2304]{1,0:T(8,128)(2,1)S(1)} collective-permute-done((bf16[128,2304]{1,0:T(8,128)(2,1)}, bf16[128,2304]{1,0:T(8,128)(2,1)S(1)}, u32[]{:S(2)}, u32[]{:S(2)}) %collective-permute-start.18) | collective-permute-done | bytes 589856 | tf_op jit(solution)/shard_map/ppermute | solution.py:286
  114.7 19.3 %collective-permute-done.40.refs_4_ = bf16[72,2304]{1,0:T(8,128)(2,1)S(1)} collective-permute-done((bf16[72,2304]{1,0:T(8,128)(2,1)S(1)}, bf16[72,2304]{1,0:T(8,128)(2,1)S(1)}, u32[]{:S(2)}, u32[]{:S(2)}) %collective-permute-start.40) | collective-permute-done | bytes 331808 | tf_op jit(solution)/shard_map/ppermute | solution.py:286
  142.2 4.1 %shard_map.173 = (bf16[72,2304]{1,0:T(8,128)(2,1)}, bf16[72,2304]{1,0:T(8,128)(2,1)}, bf16[72,2304]{1,0:T(8,128)(2,1)}, bf16[72,2304]{1,0:T(8,128)(2,1)}, bf16[7...) custom-call(f32[16,128]{1,0:T(8,128)} %get-tuple-element.126.refs_0_, ...), custom_call_target="tpu_custom_call" | custom-call | flops 679477248 | bytes 3833856 | tf_op jit(solution)/shard_map/pallas_call | solution.py:73
  149.2 14.7 %collective-permute-done.49.refs_12_ = bf16[72,2304]{1,0:T(8,128)(2,1)S(1)} collective-permute-done((bf16[72,2304]{1,0:T(8,128)(2,1)}, bf16[72,2304]{1,0:T(8,128)(2,1)S(1)}, u32[]{:S(2)}, u32[]{:S(2)}) %collective-permute-start.49) | collective-permute-done | bytes 331808 | tf_op jit(solution)/shard_map/ppermute | solution.py:286
  163.9 4.9 %collective-permute-done.50.refs_13_ = bf16[72,2304]{1,0:T(8,128)(2,1)S(1)} collective-permute-done((bf16[72,2304]{1,0:T(8,128)(2,1)}, bf16[72,2304]{1,0:T(8,128)(2,1)S(1)}, u32[]{:S(2)}, u32[]{:S(2)}) %collective-permute-start.50) | collective-permute-done | bytes 331808 | tf_op jit(solution)/shard_map/ppermute | solution.py:286
  172.5 4.1 shard_map.174
  180.1 16.2 %collective-permute-done.14.refs_4_ = bf16[72,2304]{1,0:T(8,128)(2,1)S(1)} collective-permute-done((bf16[72,2304]{1,0:T(8,128)(2,1)}, bf16[72,2304]{1,0:T(8,128)(2,1)S(1)}, u32[]{:S(2)}, u32[]{:S(2)}) %collective-permute-start.14) | collective-permute-done | bytes 331808 | tf_op jit(solution)/shard_map/ppermute | solution.py:286
  197.4 4.4 %collective-permute-done.15.refs_5_ = bf16[72,2304]{1,0:T(8,128)(2,1)S(1)} collective-permute-done((bf16[72,2304]{1,0:T(8,128)(2,1)S(1)}, bf16[72,2304]{1,0:T(8,128)(2,1)S(1)}, u32[]{:S(2)}, u32[]{:S(2)}) %collective-permute-start.15) | collective-permute-done | bytes 331808 | tf_op jit(solution)/shard_map/ppermute | solution.py:286
  207.8 36.0 %shard_map.179 = (bf16[72,2304]{1,0:T(8,128)(2,1)}, bf16[72,2304]{1,0:T(8,128)(2,1)}, bf16[72,2304]{1,0:T(8,128)(2,1)}, bf16[72,2304]{1,0:T(8,128)(2,1)}, bf16[7...) custom-call(bf16[72,2304]{1,0:T(8,128)(2,1)} %get-tuple-element.90.r, ...), custom_call_target="tpu_custom_call" | custom-call | flops 13589544960 | bytes 22118400 | tf_op jit(solution)/shard_map/pallas_call | solution.py:180
  247.1 36.0 %shard_map.175 = (bf16[72,2304]{1,0:T(8,128)(2,1)}, bf16[72,2304]{1,0:T(8,128)(2,1)}, bf16[72,2304]{1,0:T(8,128)(2,1)}, bf16[72,2304]{1,0:T(8,128)(2,1)}, bf16[7...) custom-call(bf16[72,2304]{1,0:T(8,128)(2,1)} %get-tuple-element.65.r, ...), custom_call_target="tpu_custom_call" | custom-call | flops 13589544960 | bytes 22118400 | tf_op jit(solution)/shard_map/pallas_call | solution.py:180
  288.1 19.0 %collective-permute-done.57.refs_7_ = bf16[72,2304]{1,0:T(8,128)(2,1)S(1)} collective-permute-done((bf16[72,2304]{1,0:T(8,128)(2,1)}, bf16[72,2304]{1,0:T(8,128)(2,1)S(1)}, u32[]{:S(2)}, u32[]{:S(2)}) %collective-permute-start.57) | collective-permute-done | bytes 331808 | tf_op jit(solution)/shard_map/ppermute | solution.py:286
  312.6 4.1 collective-permute-done.28.refs_5_
  318.0 15.3 %collective-permute-done.29.refs_6_ = bf16[72,2304]{1,0:T(8,128)(2,1)} collective-permute-done((bf16[72,2304]{1,0:T(8,128)(2,1)}, bf16[72,2304]{1,0:T(8,128)(2,1)}, u32[]{:S(2)}, u32[]{:S(2)}) %collective-permute-start.29) | collective-permute-done | bytes 331808 | tf_op jit(solution)/shard_map/ppermute | solution.py:286
  334.7 3.6 collective-permute-done.30.refs_7_
  340.0 4.4 %shard_map.180 = (bf16[128,2304]{1,0:T(8,128)(2,1)}, bf16[128,2304]{1,0:T(8,128)(2,1)}) custom-call(f32[16,128]{1,0:T(8,128)} %copy-done.30, f32[16,128]{1,0:T(8,128)} %copy-done.31, bf16[72,2304]{1,0:T(8,128)(2,1)} %get-tuple-element.106.refs_2_, bf16[72,2304]{1,0:T(8,128)(2,1)} %copy-done.13, bf16[72,2304]{1,0:T(8,128)(2,1)} %copy-done.14, ...), custom_call_target="tpu_custom_call" | custom-call | flops 679477248 | bytes 3833856 | tf_op jit(solution)/shard_map/pallas_call | solution.py:105
  344.5 4.6 %shard_map.176 = (f32[128,2304]{1,0:T(8,128)}, bf16[128,2304]{1,0:T(8,128)(2,1)}) custom-call(f32[16,128]{1,0:T(8,128)} %get-tuple-element.126.refs_0_, f32[16,128]{1,0:T(8,128)} %copy-done.29, bf16[72,2304]{1,0:T(8,128)(2,1)} %get-tuple-element.81.refs_2_, bf16[72,2304]{1,0:T(8,128)(2,1)} %copy-done.19, bf16[72,2304]{1,0:T(8,128)(2,1)} %copy-done.20, ...), custom_call_target="tpu_custom_call" | custom-call | flops 679477248 | bytes 3833856 | tf_op jit(solution)/shard_map/pallas_call | solution.py:105
  349.3 7.7 %collective-permute-done.6.refs_11_ = bf16[2304,128]{1,0:T(8,128)(2,1)S(1)} collective-permute-done((bf16[2304,128]{1,0:T(8,128)(2,1)S(1)}, bf16[2304,128]{1,0:T(8,128)(2,1)S(1)}, u32[]{:S(2)}, u32[]{:S(2)}) %collective-permute-start.6) | collective-permute-done | bytes 589856 | tf_op jit(solution)/shard_map/ppermute | solution.py:286
  357.0 2.7 collective-permute-start.62
  364.7 8.2 %shared.1 = f32[128,2304]{1,0:T(8,128)} custom-call(bf16[128,2304]{1,0:T(8,128)(2,1)} %refs_2_.4, bf16[128,2304]{1,0:T(8,128)(2,1)} %refs_2_.5, bf16[2304,128]{1,0:T(8,128)(2,1)} %refs_2_.3, bf16[2304,128]{1,0:T(8,128)(2,1)} %copy-done.4, bf16[2304,128]{1,0:T(8,128)(2,1)} %copy-done.5, bf16[2304,128]{1,0:T(8,128)(2,1)} %copy-done.10, ...), custom_call_target="tpu_custom_call" | custom-call | flops 1509949440 | bytes 7077888 | tf_op jit(solution)/shard_map/shared/pallas_call | solution.py:232
  372.9 2.6 collective-permute-done.62
  375.5 34.8 %collective-permute-done.61 = bf16[128,2304]{1,0:T(8,128)(2,1)S(1)} collective-permute-done((bf16[128,2304]{1,0:T(8,128)(2,1)}, bf16[128,2304]{1,0:T(8,128)(2,1)S(1)}, u32[]{:S(2)}, u32[]{:S(2)}) %collective-permute-start.61) | collective-permute-done | bytes 589856 | tf_op jit(solution)/shard_map/ppermute | solution.py:286
  410.2 2.4 add_convert_fusion
  (247 shorter events, 64.6 us)
Async XLA Ops:
  0.6 34.3 %collective-permute-start.35 = (bf16[128,2304]{1,0:T(8,128)(2,1)}, bf16[128,2304]{1,0:T(8,128)(2,1)S(1)}, u32[]{:S(2)}, u32[]{:S(2)}) collective-permute-start(bf16[128,2304]{1,0:T(8,128)(2,1)} %refs_2_.4), channel_id=1, source_target_pairs={{0,8},{1,9},{2,10},{3,11},{4,12},{5,13},{6,14},{7,15},{8,0},{9,1},... | collective-permute-start | bytes 1769480 | tf_op jit(solution)/shard_map/ppermute | solution.py:286
  3.7 33.7 %collective-permute-start.36 = (bf16[128,2304]{1,0:T(8,128)(2,1)}, bf16[128,2304]{1,0:T(8,128)(2,1)S(1)}, u32[]{:S(2)}, u32[]{:S(2)}) collective-permute-start(bf16[128,2304]{1,0:T(8,128)(2,1)} %refs_2_.4), channel_id=1, source_target_pairs={{0,24},{1,25},{2,26},{3,27},{4,28},{5,29},{6,30},{7,31},{8,16},{9,... | collective-permute-start | bytes 1769480 | tf_op jit(solution)/shard_map/ppermute | solution.py:286
  32.6 29.1 %collective-permute-start.45 = (bf16[128,2304]{1,0:T(8,128)(2,1)}, bf16[128,2304]{1,0:T(8,128)(2,1)S(1)}, u32[]{:S(2)}, u32[]{:S(2)}) collective-permute-start(bf16[128,2304]{1,0:T(8,128)(2,1)} %refs_2_.5), channel_id=1, source_target_pairs={{0,24},{1,25},{2,26},{3,27},{4,28},{5,29},{6,30},{7,31},{8,16},{9,... | collective-permute-start | bytes 1769480 | tf_op jit(solution)/shard_map/ppermute | solution.py:286
  34.6 65.3 %collective-permute-start.10 = (bf16[128,2304]{1,0:T(8,128)(2,1)}, bf16[128,2304]{1,0:T(8,128)(2,1)S(1)}, u32[]{:S(2)}, u32[]{:S(2)}) collective-permute-start(bf16[128,2304]{1,0:T(8,128)(2,1)} %refs_2_.4), channel_id=1, source_target_pairs={{0,16},{1,17},{2,18},{3,19},{4,20},{5,21},{6,22},{7,23},{8,24},{9,... | collective-permute-start | bytes 1769480 | tf_op jit(solution)/shard_map/ppermute | solution.py:286
  34.9 75.0 %collective-permute-start.18 = (bf16[128,2304]{1,0:T(8,128)(2,1)}, bf16[128,2304]{1,0:T(8,128)(2,1)S(1)}, u32[]{:S(2)}, u32[]{:S(2)}) collective-permute-start(bf16[128,2304]{1,0:T(8,128)(2,1)} %refs_2_.5), channel_id=1, source_target_pairs={{0,16},{1,17},{2,18},{3,19},{4,20},{5,21},{6,22},{7,23},{8,24},{9,... | collective-permute-start | bytes 1769480 | tf_op jit(solution)/shard_map/ppermute | solution.py:286
  37.5 74.0 %collective-permute-start = (bf16[2304,128]{1,0:T(8,128)(2,1)}, bf16[2304,128]{1,0:T(8,128)(2,1)S(1)}, u32[]{:S(2)}, u32[]{:S(2)}) collective-permute-start(bf16[2304,128]{1,0:T(8,128)(2,1)} %refs_2_.3), channel_id=1, source_target_pairs={{0,2},{1,3},{2,0},{3,1},{4,6},{5,7},{6,4},{7,5},{8,10},{9,11},{10,... | collective-permute-start | bytes 1769480 | tf_op jit(solution)/shard_map/ppermute | solution.py:286
  48.0 63.5 %collective-permute-start.37 = (bf16[72,2304]{1,0:T(8,128)(2,1)}, bf16[72,2304]{1,0:T(8,128)(2,1)S(1)}, u32[]{:S(2)}, u32[]{:S(2)}) collective-permute-start(bf16[72,2304]{1,0:T(8,128)(2,1)} %get-tuple-element.91), channel_id=1, source_target_pairs={{0,1},{1,0},{2,3},{3,2},{4,5},{5,4},{6,7},{7,6},{8,9},{9,8},{10,11... | collective-permute-start | bytes 995336 | tf_op jit(solution)/shard_map/ppermute | solution.py:286
  61.7 51.4 %collective-permute-start.38 = (bf16[72,2304]{1,0:T(8,128)(2,1)}, bf16[72,2304]{1,0:T(8,128)(2,1)S(1)}, u32[]{:S(2)}, u32[]{:S(2)}) collective-permute-start(bf16[72,2304]{1,0:T(8,128)(2,1)} %get-tuple-element.92), channel_id=1, source_target_pairs={{0,2},{1,3},{2,0},{3,1},{4,6},{5,7},{6,4},{7,5},{8,10},{9,11},{10,... | collective-permute-start | bytes 995336 | tf_op jit(solution)/shard_map/ppermute | solution.py:286
  111.6 28.2 %collective-permute-start.42 = (bf16[72,2304]{1,0:T(8,128)(2,1)S(1)}, bf16[72,2304]{1,0:T(8,128)(2,1)S(1)}, u32[]{:S(2)}, u32[]{:S(2)}) collective-permute-start(bf16[72,2304]{1,0:T(8,128)(2,1)S(1)} %copy-done.65), channel_id=1, source_target_pairs={{0,6},{1,7},{2,4},{3,5},{4,2},{5,3},{6,0},{7,1},{8,14},{9,15},{10,... | collective-permute-start | bytes 995336 | tf_op jit(solution)/shard_map/ppermute | solution.py:286
  113.1 27.9 %collective-permute-start.43 = (bf16[72,2304]{1,0:T(8,128)(2,1)S(1)}, bf16[72,2304]{1,0:T(8,128)(2,1)}, u32[]{:S(2)}, u32[]{:S(2)}) collective-permute-start(bf16[72,2304]{1,0:T(8,128)(2,1)S(1)} %copy-done.63), channel_id=1, source_target_pairs={{0,7},{1,6},{2,5},{3,4},{4,3},{5,2},{6,1},{7,0},{8,15},{9,14},{10,... | collective-permute-start | bytes 995336 | tf_op jit(solution)/shard_map/ppermute | solution.py:286
  114.5 26.4 %collective-permute-start.46 = (bf16[72,2304]{1,0:T(8,128)(2,1)}, bf16[72,2304]{1,0:T(8,128)(2,1)}, u32[]{:S(2)}, u32[]{:S(2)}) collective-permute-start(bf16[72,2304]{1,0:T(8,128)(2,1)} %get-tuple-element.99), channel_id=1, source_target_pairs={{0,1},{1,0},{2,3},{3,2},{4,5},{5,4},{6,7},{7,6},{8,9},{9,8},{10,11... | collective-permute-start | bytes 995336 | tf_op jit(solution)/shard_map/ppermute | solution.py:286
  141.0 27.9 %collective-permute-start.50 = (bf16[72,2304]{1,0:T(8,128)(2,1)}, bf16[72,2304]{1,0:T(8,128)(2,1)S(1)}, u32[]{:S(2)}, u32[]{:S(2)}) collective-permute-start(bf16[72,2304]{1,0:T(8,128)(2,1)} %get-tuple-element.103), channel_id=1, source_target_pairs={{0,5},{1,4},{2,7},{3,6},{4,1},{5,0},{6,3},{7,2},{8,13},{9,12},{10,... | collective-permute-start | bytes 995336 | tf_op jit(solution)/shard_map/ppermute | solution.py:286
  141.0 30.1 %collective-permute-start.51 = (bf16[72,2304]{1,0:T(8,128)(2,1)}, bf16[72,2304]{1,0:T(8,128)(2,1)S(1)}, u32[]{:S(2)}, u32[]{:S(2)}) collective-permute-start(bf16[72,2304]{1,0:T(8,128)(2,1)} %get-tuple-element.104), channel_id=1, source_target_pairs={{0,6},{1,7},{2,4},{3,5},{4,2},{5,3},{6,0},{7,1},{8,14},{9,15},{10,... | collective-permute-start | bytes 995336 | tf_op jit(solution)/shard_map/ppermute | solution.py:286
  146.4 30.1 %collective-permute-start.52 = (bf16[72,2304]{1,0:T(8,128)(2,1)S(1)}, bf16[72,2304]{1,0:T(8,128)(2,1)S(1)}, u32[]{:S(2)}, u32[]{:S(2)}) collective-permute-start(bf16[72,2304]{1,0:T(8,128)(2,1)S(1)} %copy-done.58), channel_id=1, source_target_pairs={{0,7},{1,6},{2,5},{3,4},{4,3},{5,2},{6,1},{7,0},{8,15},{9,14},{10,... | collective-permute-start | bytes 995336 | tf_op jit(solution)/shard_map/ppermute | solution.py:286
  148.4 28.4 %collective-permute-start.11 = (bf16[72,2304]{1,0:T(8,128)(2,1)}, bf16[72,2304]{1,0:T(8,128)(2,1)S(1)}, u32[]{:S(2)}, u32[]{:S(2)}) collective-permute-start(bf16[72,2304]{1,0:T(8,128)(2,1)} %get-tuple-element.66), channel_id=1, source_target_pairs={{0,1},{1,0},{2,3},{3,2},{4,5},{5,4},{6,7},{7,6},{8,9},{9,8},{10,11... | collective-permute-start | bytes 995336 | tf_op jit(solution)/shard_map/ppermute | solution.py:286
  176.9 26.4 %collective-permute-start.16 = (bf16[72,2304]{1,0:T(8,128)(2,1)S(1)}, bf16[72,2304]{1,0:T(8,128)(2,1)S(1)}, u32[]{:S(2)}, u32[]{:S(2)}) collective-permute-start(bf16[72,2304]{1,0:T(8,128)(2,1)S(1)} %copy-done.62), channel_id=1, source_target_pairs={{0,6},{1,7},{2,4},{3,5},{4,2},{5,3},{6,0},{7,1},{8,14},{9,15},{10,... | collective-permute-start | bytes 995336 | tf_op jit(solution)/shard_map/ppermute | solution.py:286
  201.8 42.0 %collective-permute-start.21 = (bf16[72,2304]{1,0:T(8,128)(2,1)}, bf16[72,2304]{1,0:T(8,128)(2,1)}, u32[]{:S(2)}, u32[]{:S(2)}) collective-permute-start(bf16[72,2304]{1,0:T(8,128)(2,1)} %get-tuple-element.76), channel_id=1, source_target_pairs={{0,3},{1,2},{2,1},{3,0},{4,7},{5,6},{6,5},{7,4},{8,11},{9,10},{10,... | collective-permute-start | bytes 995336 | tf_op jit(solution)/shard_map/ppermute | solution.py:286
  203.3 40.6 %collective-permute-start.22 = (bf16[72,2304]{1,0:T(8,128)(2,1)}, bf16[72,2304]{1,0:T(8,128)(2,1)}, u32[]{:S(2)}, u32[]{:S(2)}) collective-permute-start(bf16[72,2304]{1,0:T(8,128)(2,1)} %get-tuple-element.77), channel_id=1, source_target_pairs={{0,4},{1,5},{2,6},{3,7},{4,0},{5,1},{6,2},{7,3},{8,12},{9,13},{10,... | collective-permute-start | bytes 995336 | tf_op jit(solution)/shard_map/ppermute | solution.py:286
  204.6 39.8 %collective-permute-start.23 = (bf16[72,2304]{1,0:T(8,128)(2,1)}, bf16[72,2304]{1,0:T(8,128)(2,1)}, u32[]{:S(2)}, u32[]{:S(2)}) collective-permute-start(bf16[72,2304]{1,0:T(8,128)(2,1)} %get-tuple-element.78), channel_id=1, source_target_pairs={{0,5},{1,4},{2,7},{3,6},{4,1},{5,0},{6,3},{7,2},{8,13},{9,12},{10,... | collective-permute-start | bytes 995336 | tf_op jit(solution)/shard_map/ppermute | solution.py:286
  204.6 40.8 %collective-permute-start.24 = (bf16[72,2304]{1,0:T(8,128)(2,1)}, bf16[72,2304]{1,0:T(8,128)(2,1)}, u32[]{:S(2)}, u32[]{:S(2)}) collective-permute-start(bf16[72,2304]{1,0:T(8,128)(2,1)} %get-tuple-element.79), channel_id=1, source_target_pairs={{0,6},{1,7},{2,4},{3,5},{4,2},{5,3},{6,0},{7,1},{8,14},{9,15},{10,... | collective-permute-start | bytes 995336 | tf_op jit(solution)/shard_map/ppermute | solution.py:286
  205.9 39.9 %collective-permute-start.25 = (bf16[72,2304]{1,0:T(8,128)(2,1)}, bf16[72,2304]{1,0:T(8,128)(2,1)}, u32[]{:S(2)}, u32[]{:S(2)}) collective-permute-start(bf16[72,2304]{1,0:T(8,128)(2,1)} %get-tuple-element.80), channel_id=1, source_target_pairs={{0,7},{1,6},{2,5},{3,4},{4,3},{5,2},{6,1},{7,0},{8,15},{9,14},{10,... | collective-permute-start | bytes 995336 | tf_op jit(solution)/shard_map/ppermute | solution.py:286
  243.8 39.3 %collective-permute-start.1 = (bf16[2304,128]{1,0:T(8,128)(2,1)S(1)}, bf16[2304,128]{1,0:T(8,128)(2,1)S(1)}, u32[]{:S(2)}, u32[]{:S(2)}) collective-permute-start(bf16[2304,128]{1,0:T(8,128)(2,1)S(1)} %copy-done.1), channel_id=1, source_target_pairs={{0,1},{1,0},{2,3},{3,2},{4,5},{5,4},{6,7},{7,6},{8,9},{9,8},{10,11... | collective-permute-start | bytes 1769480 | tf_op jit(solution)/shard_map/ppermute | solution.py:286
  243.9 40.1 %collective-permute-start.53 = (bf16[72,2304]{1,0:T(8,128)(2,1)}, bf16[72,2304]{1,0:T(8,128)(2,1)S(1)}, u32[]{:S(2)}, u32[]{:S(2)}) collective-permute-start(bf16[72,2304]{1,0:T(8,128)(2,1)} %get-tuple-element.107), channel_id=1, source_target_pairs={{0,1},{1,0},{2,3},{3,2},{4,5},{5,4},{6,7},{7,6},{8,9},{9,8},{10,11... | collective-permute-start | bytes 995336 | tf_op jit(solution)/shard_map/ppermute | solution.py:286
  244.4 40.9 %collective-permute-start.54 = (bf16[72,2304]{1,0:T(8,128)(2,1)}, bf16[72,2304]{1,0:T(8,128)(2,1)S(1)}, u32[]{:S(2)}, u32[]{:S(2)}) collective-permute-start(bf16[72,2304]{1,0:T(8,128)(2,1)} %get-tuple-element.108), channel_id=1, source_target_pairs={{0,2},{1,3},{2,0},{3,1},{4,6},{5,7},{6,4},{7,5},{8,10},{9,11},{10,... | collective-permute-start | bytes 995336 | tf_op jit(solution)/shard_map/ppermute | solution.py:286
  245.5 40.9 %collective-permute-start.55 = (bf16[72,2304]{1,0:T(8,128)(2,1)}, bf16[72,2304]{1,0:T(8,128)(2,1)S(1)}, u32[]{:S(2)}, u32[]{:S(2)}) collective-permute-start(bf16[72,2304]{1,0:T(8,128)(2,1)} %get-tuple-element.109), channel_id=1, source_target_pairs={{0,3},{1,2},{2,1},{3,0},{4,7},{5,6},{6,5},{7,4},{8,11},{9,10},{10,... | collective-permute-start | bytes 995336 | tf_op jit(solution)/shard_map/ppermute | solution.py:286
  245.8 41.2 %collective-permute-start.56 = (bf16[72,2304]{1,0:T(8,128)(2,1)}, bf16[72,2304]{1,0:T(8,128)(2,1)}, u32[]{:S(2)}, u32[]{:S(2)}) collective-permute-start(bf16[72,2304]{1,0:T(8,128)(2,1)} %get-tuple-element.110), channel_id=1, source_target_pairs={{0,4},{1,5},{2,6},{3,7},{4,0},{5,1},{6,2},{7,3},{8,12},{9,13},{10,... | collective-permute-start | bytes 995336 | tf_op jit(solution)/shard_map/ppermute | solution.py:286
  309.3 29.1 %collective-permute-start.30 = (bf16[72,2304]{1,0:T(8,128)(2,1)}, bf16[72,2304]{1,0:T(8,128)(2,1)}, u32[]{:S(2)}, u32[]{:S(2)}) collective-permute-start(bf16[72,2304]{1,0:T(8,128)(2,1)} %get-tuple-element.86), channel_id=1, source_target_pairs={{0,5},{1,4},{2,7},{3,6},{4,1},{5,0},{6,3},{7,2},{8,13},{9,12},{10,... | collective-permute-start | bytes 995336 | tf_op jit(solution)/shard_map/ppermute | solution.py:286
  309.4 30.0 %collective-permute-start.31 = (bf16[72,2304]{1,0:T(8,128)(2,1)}, bf16[72,2304]{1,0:T(8,128)(2,1)}, u32[]{:S(2)}, u32[]{:S(2)}) collective-permute-start(bf16[72,2304]{1,0:T(8,128)(2,1)} %get-tuple-element.87), channel_id=1, source_target_pairs={{0,6},{1,7},{2,4},{3,5},{4,2},{5,3},{6,0},{7,1},{8,14},{9,15},{10,... | collective-permute-start | bytes 995336 | tf_op jit(solution)/shard_map/ppermute | solution.py:286
  311.1 28.4 %collective-permute-start.32 = (bf16[72,2304]{1,0:T(8,128)(2,1)}, bf16[72,2304]{1,0:T(8,128)(2,1)}, u32[]{:S(2)}, u32[]{:S(2)}) collective-permute-start(bf16[72,2304]{1,0:T(8,128)(2,1)} %get-tuple-element.88), channel_id=1, source_target_pairs={{0,7},{1,6},{2,5},{3,4},{4,3},{5,2},{6,1},{7,0},{8,15},{9,14},{10,... | collective-permute-start | bytes 995336 | tf_op jit(solution)/shard_map/ppermute | solution.py:286
  316.7 32.5 %collective-permute-start.3 = (bf16[2304,128]{1,0:T(8,128)(2,1)S(1)}, bf16[2304,128]{1,0:T(8,128)(2,1)S(1)}, u32[]{:S(2)}, u32[]{:S(2)}) collective-permute-start(bf16[2304,128]{1,0:T(8,128)(2,1)S(1)} %copy-done.2), channel_id=1, source_target_pairs={{0,2},{1,3},{2,0},{3,1},{4,6},{5,7},{6,4},{7,5},{8,10},{9,11},{10,... | collective-permute-start | bytes 1769480 | tf_op jit(solution)/shard_map/ppermute | solution.py:286
  359.7 50.5 %collective-permute-start.61 = (bf16[128,2304]{1,0:T(8,128)(2,1)}, bf16[128,2304]{1,0:T(8,128)(2,1)S(1)}, u32[]{:S(2)}, u32[]{:S(2)}) collective-permute-start(bf16[128,2304]{1,0:T(8,128)(2,1)} %get-tuple-element.115), channel_id=1, source_target_pairs={{0,16},{1,17},{2,18},{3,19},{4,20},{5,21},{6,22},{7,23},{8,24},{9,... | collective-permute-start | bytes 1769480 | tf_op jit(solution)/shard_map/ppermute | solution.py:286
  359.7 50.5 %collective-permute-start.60 = (bf16[128,2304]{1,0:T(8,128)(2,1)S(1)}, bf16[128,2304]{1,0:T(8,128)(2,1)S(1)}, u32[]{:S(2)}, u32[]{:S(2)}) collective-permute-start(bf16[128,2304]{1,0:T(8,128)(2,1)S(1)} %copy-done.34), channel_id=1, source_target_pairs={{0,8},{1,9},{2,10},{3,11},{4,12},{5,13},{6,14},{7,15},{8,0},{9,1},... | collective-permute-start | bytes 1769480 | tf_op jit(solution)/shard_map/ppermute | solution.py:286
  (99 other events, 2469.4 us)
where the time goes:
time: 413 us
  waiting for transfers between devices  228 us (55%)
  Pallas kernels  106 us (26%)
  starting transfers between devices  69.7 us (17%)
  other arithmetic  6.01 us (1%)
    ppermute x63, waiting for transfers between devices, swap(): return lax.ppermute(array, AXES, [(i, i ^ step) for i in range(owners)])  228 us
    pallas_call x2, Pallas kernels, expert(): pl.pallas_call(functools.partial(expert_kernel, peers, steps), grid=(step...  72 us
    ppermute x63, starting transfers between devices, swap(): return lax.ppermute(array, AXES, [(i, i ^ step) for i in range(owners)])  69.7 us
    pallas_call x4, Pallas kernels, pack(): pl.pallas_call(functools.partial(pack_kernel, peers, cap, count, scaled),...  16.6 us
    pallas_call x2, Pallas kernels, merge(): pl.pallas_call(functools.partial(merge_kernel, peers, cap, count), grid=(...  9.04 us
  transfers between devices with their start and end apart: 63, of which 19 were waited for; matrix products, arithmetic and copies ran while one was open for 1% of the time, Pallas kernels for 26%

commit v1 on v0

--- a/solution.py
+++ b/solution.py
@@ -53,6 +53,10 @@
     return jnp.concatenate(hot, axis=0), scale
 
 
+def tile_of(width):
+    return 768 if width % 768 == 0 else width
+
+
 def pack_kernel(peers, cap, count, scaled, *refs):
     info_refs, block_refs, out_refs = refs[:count], refs[count : 2 * count], refs[2 * count :]
     hot, scale = selection(info_refs, peers, cap, scaled)
@@ -66,14 +70,18 @@
 
 def pack(infos, blocks, peers, cap, scaled):
     count = len(infos)
-    tokens, width = blocks[0].shape
-    tile = width // 3 if width % 384 == 0 else width
+    tokens = infos[0].shape[1]
+    width = min(array.shape[1] for array, _ in blocks)
+    tile = tile_of(width)
     whole = pl.BlockSpec(infos[0].shape, lambda i: (0, 0))
-    part = pl.BlockSpec((tokens, tile), lambda i: (0, i))
+    parts = [
+        pl.BlockSpec((tokens, tile), functools.partial(lambda at, i: (0, i + at), start // tile))
+        for _, start in blocks
+    ]
     return pl.pallas_call(
         functools.partial(pack_kernel, peers, cap, count, scaled),
         grid=(width // tile,),
-        in_specs=[whole] * count + [part] * count,
+        in_specs=[whole] * count + parts,
         out_specs=[pl.BlockSpec((count * cap, tile), lambda i: (0, i))] * peers,
         out_shape=[jax.ShapeDtypeStruct((count * cap, width), BF16)] * peers,
         compiler_params=params(),
@@ -82,7 +90,7 @@
             bytes_accessed=2 * width * (peers * count * cap + count * tokens),
             transcendentals=0,
         ),
-    )(*infos, *blocks)
+    )(*infos, *[array for array, _ in blocks])
 
 
 def merge_kernel(peers, cap, count, *refs):
@@ -100,7 +108,7 @@
     count = len(infos)
     tokens = infos[0].shape[1]
     width = back[0].shape[1]
-    tile = width // 3 if width % 384 == 0 else width
+    tile = tile_of(width)
     whole = pl.BlockSpec(infos[0].shape, lambda i: (0, 0))
     return pl.pallas_call(
         functools.partial(merge_kernel, peers, cap, count),
@@ -117,32 +125,49 @@
     )(*infos, *back)
 
 
-def expert_kernel(peers, steps, *refs):
-    row_refs, grad_refs = refs[:peers], refs[peers : 2 * peers]
-    gate_w, up_w, down_w, gate_in, gate_out, up_in, up_out = refs[2 * peers : 2 * peers + 7]
-    out_refs = refs[2 * peers + 7 : 3 * peers + 7]
-    gate_in_grad, gate_out_grad, up_in_grad, up_out_grad = refs[3 * peers + 7 : 3 * peers + 11]
-    rows, grads, total, low_gate, low_up, back_gate, back_up = refs[3 * peers + 11 :]
+def expert_kernel(peers, steps, pieces, *refs):
+    refs = list(refs)
+
+    def take(count):
+        taken, refs[:count] = refs[:count], []
+        return taken
+
+    row_refs, grad_refs = ([take(peers) for _ in range(n)] for n in pieces[:2])
+    gate_w, up_w, down_w, gate_in, gate_out, up_in, up_out = take(7)
+    out_refs = [take(peers) for _ in range(pieces[2])]
+    gate_in_grad, gate_out_grad, up_in_grad, up_out_grad = take(4)
+    rows, grads, total, low, maps_in, back = refs
     step = pl.program_id(0)
-    height = row_refs[0].shape[0]
+    height = row_refs[0][0].shape[0]
+    rank = gate_in.shape[0]
+
+    def gather(target, groups):
+        at = 0
+        for group in groups:
+            wide = group[0].shape[1]
+            target[:, at : at + wide] = jnp.concatenate(
+                [r[...].astype(F32) for r in group], axis=0
+            ).astype(BF16)
+            at += wide
 
     @pl.when(step == 0)
     def _():
-        rows[...] = jnp.concatenate([r[...].astype(F32) for r in row_refs], axis=0).astype(BF16)
-        grads[...] = jnp.concatenate([r[...].astype(F32) for r in grad_refs], axis=0).astype(BF16)
-        low_gate[...] = dot(rows[...], gate_in[...], 1, 1).astype(BF16)
-        low_up[...] = dot(rows[...], up_in[...], 1, 1).astype(BF16)
-        back_gate[...] = jnp.zeros_like(back_gate)
-        back_up[...] = jnp.zeros_like(back_up)
-
-    gate_pre = dot(rows[...], gate_w[...], 1, 0) + dot(low_gate[...], gate_out[...], 1, 0)
-    up_pre = dot(rows[...], up_w[...], 1, 0) + dot(low_up[...], up_out[...], 1, 0)
+        gather(rows, row_refs)
+        gather(grads, grad_refs)
+        maps_in[:rank] = gate_in[...]
+        maps_in[rank:] = up_in[...]
+        low[...] = dot(rows[...], maps_in[...], 1, 1).astype(BF16)
+        back[...] = jnp.zeros_like(back)
+
+    low_gate, low_up = low[:, :rank], low[:, rank:]
+    gate_pre = dot(rows[...], gate_w[...], 1, 0) + dot(low_gate, gate_out[...], 1, 0)
+    up_pre = dot(rows[...], up_w[...], 1, 0) + dot(low_up, up_out[...], 1, 0)
     d_hidden = dot(grads[...], down_w[...], 1, 1)
     d_gate, d_up = cotangents(gate_pre, up_pre, d_hidden)
-    back_gate[...] += dot(d_gate, gate_out[...], 1, 1)
-    back_up[...] += dot(d_up, up_out[...], 1, 1)
-    gate_out_grad[...] = dot(low_gate[...], d_gate, 0, 0)
-    up_out_grad[...] = dot(low_up[...], d_up, 0, 0)
+    back[:, :rank] += dot(d_gate, gate_out[...], 1, 1)
+    back[:, rank:] += dot(d_up, up_out[...], 1, 1)
+    gate_out_grad[...] = dot(low_gate, d_gate, 0, 0)
+    up_out_grad[...] = dot(low_up, d_up, 0, 0)
     part = dot(d_gate, gate_w[...], 1, 1) + dot(d_up, up_w[...], 1, 1)
 
     @pl.when(step == 0)
@@ -155,35 +180,44 @@
 
     @pl.when(step == steps - 1)
     def _():
-        low_dgate = back_gate[...].astype(BF16)
-        low_dup = back_up[...].astype(BF16)
-        done = total[...] + dot(low_dgate, gate_in[...], 1, 0) + dot(low_dup, up_in[...], 1, 0)
-        for d in range(peers):
-            out_refs[d][...] = done[d * height : (d + 1) * height].astype(BF16)
-        gate_in_grad[...] = dot(low_dgate, rows[...], 0, 0)
-        up_in_grad[...] = dot(low_dup, rows[...], 0, 0)
-
-
-def expert(rows, grads, weights):
-    peers = len(rows)
-    height, width = rows[0].shape
+        low_back = back[...].astype(BF16)
+        done = total[...] + dot(low_back, maps_in[...], 1, 0)
+        at = 0
+        for group in out_refs:
+            wide = group[0].shape[1]
+            for d in range(peers):
+                group[d][...] = done[d * height : (d + 1) * height, at : at + wide].astype(BF16)
+            at += wide
+        in_grads = dot(low_back, rows[...], 0, 0)
+        gate_in_grad[...] = in_grads[:rank]
+        up_in_grad[...] = in_grads[rank:]
+
+
+def expert(rows, grads, weights, out_widths):
+    peers = len(rows[0])
+    height = rows[0][0].shape[0]
     gate_w, _, _, gate_in, _, _, _ = weights
-    hidden = gate_w.shape[1]
+    width, hidden = gate_w.shape
     rank = gate_in.shape[0]
-    tile = 256 if hidden % 256 == 0 else hidden
+    tile = 512 if hidden % 512 == 0 else hidden
     steps = hidden // tile
     count = peers * height
-    block = pl.BlockSpec((height, width), lambda i: (0, 0))
+
+    def block(wide):
+        return pl.BlockSpec((height, wide), lambda i: (0, 0))
+
+    inputs = [array for group in rows + grads for array in group]
     wide = pl.BlockSpec((width, tile), lambda i: (0, i))
     low_in = pl.BlockSpec((rank, width), lambda i: (0, 0))
     low_out = pl.BlockSpec((rank, tile), lambda i: (0, i))
-    return pl.pallas_call(
-        functools.partial(expert_kernel, peers, steps),
+    result = pl.pallas_call(
+        functools.partial(expert_kernel, peers, steps, (len(rows), len(grads), len(out_widths))),
         grid=(steps,),
-        in_specs=[block] * (2 * peers)
+        in_specs=[block(array.shape[1]) for array in inputs]
         + [wide, wide, pl.BlockSpec((tile, width), lambda i: (i, 0)), low_in, low_out, low_in, low_out],
-        out_specs=[block] * peers + [low_in, low_out, low_in, low_out],
-        out_shape=[jax.ShapeDtypeStruct((height, width), BF16)] * peers
+        out_specs=[block(w) for w in out_widths for _ in range(peers)]
+        + [low_in, low_out, low_in, low_out],
+        out_shape=[jax.ShapeDtypeStruct((height, w), BF16) for w in out_widths for _ in range(peers)]
         + [
             jax.ShapeDtypeStruct((rank, width), F32),
             jax.ShapeDtypeStruct((rank, hidden), F32),
@@ -194,10 +228,9 @@
             pltpu.VMEM((count, width), BF16),
             pltpu.VMEM((count, width), BF16),
             pltpu.VMEM((count, width), F32),
-            pltpu.VMEM((count, rank), BF16),
-            pltpu.VMEM((count, rank), BF16),
-            pltpu.VMEM((count, rank), F32),
-            pltpu.VMEM((count, rank), F32),
+            pltpu.VMEM((count, 2 * rank), BF16),
+            pltpu.VMEM((2 * rank, width), BF16),
+            pltpu.VMEM((count, 2 * rank), F32),
         ],
         compiler_params=params(60),
         cost_estimate=pl.CostEstimate(
@@ -205,7 +238,42 @@
             bytes_accessed=6 * width * (count + hidden),
             transcendentals=count * hidden,
         ),
-    )(*rows, *grads, *weights)
+    )(*inputs, *weights)
+    outs = [result[i * peers : (i + 1) * peers] for i in range(len(out_widths))]
+    return outs, result[-4:]
+
+
+def finish(base, terms):
+    def kernel(*refs):
+        base_ref, out = refs[0], refs[-1]
+        at = 1
+        pieces = []
+        for term in terms:
+            start = 0
+            for piece in term:
+                pieces.append((start, start + piece.shape[1], refs[at]))
+                start += piece.shape[1]
+                at += 1
+        edges = sorted({0} | {hi for _, hi, _ in pieces})
+        for lo, hi in zip(edges, edges[1:]):
+            value = base_ref[:, lo:hi]
+            for start, stop, ref in pieces:
+                if start <= lo and hi <= stop:
+                    value = value + ref[:, lo - start : hi - start].astype(F32)
+            out[:, lo:hi] = value.astype(BF16)
+
+    flat = [piece for term in terms for piece in term]
+    return pl.pallas_call(
+        kernel,
+        out_shape=jax.ShapeDtypeStruct(base.shape, BF16),
+        compiler_params=params(),
+        cost_estimate=pl.CostEstimate(
+            flops=base.size * (len(terms) + 1),
+            bytes_accessed=base.size * (6 + 2 * len(terms)),
+            transcendentals=0,
+        ),
+        name="finish",
+    )(base, *flat)
 
 
 def shared_kernel(slices, *refs):
@@ -252,6 +320,14 @@
 
 def plane_groups(planes):
     return [list(range(0, planes, 2)), list(range(1, planes, 2))]
+
+
+def widths(width, pieces):
+    return [width // pieces] * pieces if width % (768 * pieces) == 0 else [width]
+
+
+IN_PIECES = 3
+OUT_PIECES = 3
 
 
 def local(
@@ -274,7 +350,7 @@
     owners = lax.axis_size("ep") * rep_count
     peers = 2 * rep_count
     planes = owners // peers
-    token_rows, _ = tokens.shape
+    token_rows, model_width = tokens.shape
     pick_count = chosen_experts.shape[1]
     cap = token_rows * pick_count * 9 // (8 * owners)
     me = lax.axis_index(AXES)
@@ -301,12 +377,9 @@
 
     groups = plane_groups(planes)
     infos = {p: swap(info[p], p, 0) for p in range(planes)}
-    token_blocks, grad_blocks = {}, {}
-    for group in groups:
-        for p in group:
-            token_blocks[p] = swap(tokens, p, 0)
-        for p in group:
-            grad_blocks[p] = swap(output_grad, p, 0)
+    every = [model_width]
+    in_widths = widths(model_width, IN_PIECES)
+    out_widths = widths(model_width, OUT_PIECES)
 
     weights = (
         gate_weight[0],
@@ -322,25 +395,43 @@
         for kind, held in slices.items():
             slices[kind] = held + [swap(piece, 0, bit) for piece in held]
 
-    parts = {}
+    def pieces(array, p, sizes):
+        if p == 0:
+            return [(array, sum(sizes[:c])) for c in range(len(sizes))]
+        found = []
+        for c, size in enumerate(sizes):
+            start = sum(sizes[:c])
+            found.append((swap(array[:, start : start + size], p, 0), 0))
+        return found
+
+    def fan_out(arrays):
+        return [swap(arrays[d], 0, d) for d in range(peers)]
+
+    terms = []
     adapter = []
-    for group in groups:
+    for g, group in enumerate(groups):
         seen = [infos[p] for p in group]
-        row_out = pack(seen, [token_blocks[p] for p in group], peers, cap, False)
-        grad_out = pack(seen, [grad_blocks[p] for p in group], peers, cap, True)
-        rows = [swap(row_out[d], 0, d) for d in range(peers)]
-        grads = [swap(grad_out[d], 0, d) for d in range(peers)]
-        result = expert(rows, grads, weights)
-        adapter.append(result[peers:])
-        back = [swap(result[d], 0, d) for d in range(peers)]
-        kinds = [F32 if p == 0 else BF16 for p in group]
-        merged = merge(seen, back, peers, cap, kinds)
-        for p, part in zip(group, merged):
-            parts[p] = swap(part, p, 0)
-    total = shared(tokens, output_grad, *slices.values())
-    for p in range(planes):
-        total = total + parts[p].astype(F32)
-    token_grad = total.astype(BF16)
+        sizes, out_sizes = (in_widths, every) if g == 0 else (every, out_widths)
+        blocks = [pieces(tokens, p, sizes) for p in group]
+        rows = []
+        for c in range(len(sizes)):
+            packed = pack(seen, [block[c] for block in blocks], peers, cap, False)
+            rows.append(fan_out(packed))
+        blocks = [pieces(output_grad, p, every) for p in group]
+        packed = pack(seen, [block[0] for block in blocks], peers, cap, True)
+        grads = [fan_out(packed)]
+        outs, grads_of_maps = expert(rows, grads, weights, out_sizes)
+        adapter.append(grads_of_maps)
+        found = {p: [] for p in group}
+        for out in outs:
+            back = fan_out(out)
+            kinds = [F32 if p == 0 else BF16 for p in group]
+            merged = merge(seen, back, peers, cap, kinds)
+            for p, part in zip(group, merged):
+                found[p].append(swap(part, p, 0))
+        terms += list(found.values())
+    base = shared(tokens, output_grad, *slices.values())
+    token_grad = finish(base, terms)
     adapter_grads = [sum(pieces[1:], pieces[0])[None] for pieces in zip(*adapter)]
     return (token_grad, *adapter_grads)
 

time: 413 us -> 418 us (1.012); the launches traced: 413 us -> 412 us
  starting transfers between devices: 69.7 us -> 103 us
  waiting for transfers between devices: 228 us -> 204 us
  Pallas kernels: 106 us -> 95.4 us
    ppermute x63 -> x97, starting transfers between devices: 69.7 us -> 103 us  [swap(): return lax.ppermute(array, AXES, [(i, i ^ step) for i in range(owners)])]
    ppermute x63 -> x97, waiting for transfers between devices: 228 us -> 204 us  [swap(): return lax.ppermute(array, AXES, [(i, i ^ step) for i in range(owners)])]
    pallas_call x2 -> x3, Pallas kernels: 72 us -> 55.8 us  [the longest x2 52.6 us: expert(): pl.pallas_call(functools.partial(expert_kernel, peers, steps, (len(rows),...]
    pallas_call x2 -> x4, Pallas kernels: 9.04 us -> 12.4 us  [merge(): pl.pallas_call(functools.partial(merge_kernel, peers, cap, count), grid=(...]
    pallas_call x4 -> x6, Pallas kernels: 16.6 us -> 19 us  [pack(): pl.pallas_call(functools.partial(pack_kernel, peers, cap, count, scaled),...]
  transfers between devices with their start and end apart: 63 -> 97, of which waited for: 19 -> 29; matrix products, arithmetic and copies ran while one was open for 1% -> 1% of each run, Pallas kernels for 26% -> 22%
where the time goes in v1:
time: 418 us; the launch traced here: 412 us
  waiting for transfers between devices  204 us (49%)
  starting transfers between devices  103 us (25%)
  Pallas kernels  95.4 us (23%)
  other arithmetic  4.62 us (1%)
    ppermute x97, waiting for transfers between devices, swap(): return lax.ppermute(array, AXES, [(i, i ^ step) for i in range(owners)])  204 us
    ppermute x97, starting transfers between devices, swap(): return lax.ppermute(array, AXES, [(i, i ^ step) for i in range(owners)])  103 us
    pallas_call x2, Pallas kernels, expert(): pl.pallas_call(functools.partial(expert_kernel, peers, steps, (len(rows),...  52.6 us
    pallas_call x6, Pallas kernels, pack(): pl.pallas_call(functools.partial(pack_kernel, peers, cap, count, scaled),...  19 us
    pallas_call x4, Pallas kernels, merge(): pl.pallas_call(functools.partial(merge_kernel, peers, cap, count), grid=(...  12.4 us
  transfers between devices with their start and end apart: 97, of which 29 were waited for; matrix products, arithmetic and copies ran while one was open for 1% of the time, Pallas kernels for 22%

profile of v1, /device:TPU:0, one launch (start us, length us, event | category | flops | bytes accessed | tf_op | source)
XLA Modules:
  0.0 412.5 jit_solution(6587622771160001969)
XLA Ops:
  1.8 4.1 %collective-permute-start.10 = (bf16[128,768]{1,0:T(8,128)(2,1)S(1)}, bf16[128,768]{1,0:T(8,128)(2,1)S(1)}, u32[]{:S(2)}, u32[]{:S(2)}) collective-permute-start(bf16[128,768]{1,0:T(8,128)(2,1)S(1)} %get-tuple-element.199), channel_id=1, source_target_pairs={{0,16},{1,17},{2,18},{3,19},{4,20},{5,21},{6,22},{7,23},{8,24},{9,... | collective-permute-start | bytes 589832 | tf_op jit(solution)/shard_map/ppermute | solution.py:362
  6.0 2.8 collective-permute-start.26
  13.1 19.1 %collective-permute-done.9.refs_1_ = f32[16,128]{1,0:T(8,128)S(1)} collective-permute-done((f32[16,128]{1,0:T(8,128)S(1)}, f32[16,128]{1,0:T(8,128)S(1)}, u32[]{:S(2)}, u32[]{:S(2)}) %collective-permute-start.9) | collective-permute-done | bytes 8224 | tf_op jit(solution)/shard_map/ppermute | solution.py:362
  32.2 3.5 collective-permute-start.51
  42.4 2.5 collective-permute-done.12.refs_2_
  54.8 2.6 collective-permute-done.20.refs_10_
  62.8 3.1 collective-permute-start.53
  68.6 3.3 collective-permute-done.28.refs_18_
  75.8 6.3 %collective-permute-done.31.refs_21_ = bf16[72,768]{1,0:T(8,128)(2,1)S(1)} collective-permute-done((bf16[72,768]{1,0:T(8,128)(2,1)}, bf16[72,768]{1,0:T(8,128)(2,1)S(1)}, u32[]{:S(2)}, u32[]{:S(2)}) %collective-permute-start.31) | collective-permute-done | bytes 110624 | tf_op jit(solution)/shard_map/ppermute | solution.py:362
  87.8 22.1 %collective-permute-done.61.refs_2_ = bf16[128,2304]{1,0:T(8,128)(2,1)S(1)} collective-permute-done((bf16[128,2304]{1,0:T(8,128)(2,1)}, bf16[128,2304]{1,0:T(8,128)(2,1)S(1)}, u32[]{:S(2)}, u32[]{:S(2)}) %collective-permute-start.61) | collective-permute-done | bytes 589856 | tf_op jit(solution)/shard_map/ppermute | solution.py:362
  110.7 32.6 %collective-permute-done.34.refs_3_ = bf16[128,2304]{1,0:T(8,128)(2,1)S(1)} collective-permute-done((bf16[128,2304]{1,0:T(8,128)(2,1)}, bf16[128,2304]{1,0:T(8,128)(2,1)S(1)}, u32[]{:S(2)}, u32[]{:S(2)}) %collective-permute-start.34) | collective-permute-done | bytes 589856 | tf_op jit(solution)/shard_map/ppermute | solution.py:362
  143.9 4.3 %shard_map.179 = (bf16[72,2304]{1,0:T(8,128)(2,1)}, bf16[72,2304]{1,0:T(8,128)(2,1)}, bf16[72,2304]{1,0:T(8,128)(2,1)}, bf16[72,2304]{1,0:T(8,128)(2,1)}, bf16[7...) custom-call(f32[16,128]{1,0:T(8,128)} %copy-done.46, ...), custom_call_target="tpu_custom_call" | custom-call | flops 679477248 | bytes 3833856 | tf_op jit(solution)/shard_map/pallas_call | solution.py:81
  154.0 4.1 shard_map.180
  160.0 5.4 %collective-permute-done.56.refs_3_ = bf16[72,2304]{1,0:T(8,128)(2,1)S(1)} collective-permute-done((bf16[72,2304]{1,0:T(8,128)(2,1)}, bf16[72,2304]{1,0:T(8,128)(2,1)S(1)}, u32[]{:S(2)}, u32[]{:S(2)}) %collective-permute-start.56) | collective-permute-done | bytes 331808 | tf_op jit(solution)/shard_map/ppermute | solution.py:362
  167.8 13.1 %collective-permute-done.58.refs_5_ = bf16[72,2304]{1,0:T(8,128)(2,1)S(1)} collective-permute-done((bf16[72,2304]{1,0:T(8,128)(2,1)}, bf16[72,2304]{1,0:T(8,128)(2,1)S(1)}, u32[]{:S(2)}, u32[]{:S(2)}) %collective-permute-start.58) | collective-permute-done | bytes 331808 | tf_op jit(solution)/shard_map/ppermute | solution.py:362
  184.2 4.0 shard_map.176
  196.3 16.5 %collective-permute-done.67.refs_13_ = bf16[72,2304]{1,0:T(8,128)(2,1)S(1)} collective-permute-done((bf16[72,2304]{1,0:T(8,128)(2,1)}, bf16[72,2304]{1,0:T(8,128)(2,1)S(1)}, u32[]{:S(2)}, u32[]{:S(2)}) %collective-permute-start.67) | collective-permute-done | bytes 331808 | tf_op jit(solution)/shard_map/ppermute | solution.py:362
  219.0 26.6 %shard_map.181 = (bf16[72,768]{1,0:T(8,128)(2,1)}, bf16[72,768]{1,0:T(8,128)(2,1)}, bf16[72,768]{1,0:T(8,128)(2,1)}, bf16[72,768]{1,0:T(8,128)(2,1)}, bf16[72,76...) custom-call(bf16[72,2304]{1,0:T(8,128)(2,1)} %get-tuple-element.143., ...), custom_call_target="tpu_custom_call" | custom-call | flops 13589544960 | bytes 22118400 | tf_op jit(solution)/shard_map/pallas_call | solution.py:213
  255.4 4.0 collective-permute-done.90.refs_7_
  265.7 26.0 %shard_map.177 = (bf16[72,2304]{1,0:T(8,128)(2,1)}, bf16[72,2304]{1,0:T(8,128)(2,1)}, bf16[72,2304]{1,0:T(8,128)(2,1)}, bf16[72,2304]{1,0:T(8,128)(2,1)}, bf16[7...) custom-call(bf16[72,768]{1,0:T(8,128)(2,1)} %get-tuple-element.101.r, ...), custom_call_target="tpu_custom_call" | custom-call | flops 13589544960 | bytes 22118400 | tf_op jit(solution)/shard_map/pallas_call | solution.py:213
  295.8 16.1 %collective-permute-done.71.refs_4_ = bf16[72,768]{1,0:T(8,128)(2,1)S(1)} collective-permute-done((bf16[72,768]{1,0:T(8,128)(2,1)}, bf16[72,768]{1,0:T(8,128)(2,1)S(1)}, u32[]{:S(2)}, u32[]{:S(2)}) %collective-permute-start.71) | collective-permute-done | bytes 110624 | tf_op jit(solution)/shard_map/ppermute | solution.py:362
  311.9 5.3 %collective-permute-done.72.refs_5_ = bf16[72,768]{1,0:T(8,128)(2,1)S(1)} collective-permute-done((bf16[72,768]{1,0:T(8,128)(2,1)}, bf16[72,768]{1,0:T(8,128)(2,1)S(1)}, u32[]{:S(2)}, u32[]{:S(2)}) %collective-permute-start.72) | collective-permute-done | bytes 110624 | tf_op jit(solution)/shard_map/ppermute | solution.py:362
  321.6 20.7 %collective-permute-done.45.refs_6_ = bf16[72,2304]{1,0:T(8,128)(2,1)S(1)} collective-permute-done((bf16[72,2304]{1,0:T(8,128)(2,1)}, bf16[72,2304]{1,0:T(8,128)(2,1)S(1)}, u32[]{:S(2)}, u32[]{:S(2)}) %collective-permute-start.45) | collective-permute-done | bytes 331808 | tf_op jit(solution)/shard_map/ppermute | solution.py:362
  343.7 4.7 %collective-permute-done.46.refs_7_ = bf16[72,2304]{1,0:T(8,128)(2,1)S(1)} collective-permute-done((bf16[72,2304]{1,0:T(8,128)(2,1)}, bf16[72,2304]{1,0:T(8,128)(2,1)S(1)}, u32[]{:S(2)}, u32[]{:S(2)}) %collective-permute-start.46) | collective-permute-done | bytes 331808 | tf_op jit(solution)/shard_map/ppermute | solution.py:362
  354.2 4.8 %shard_map.178 = (f32[128,2304]{1,0:T(8,128)}, bf16[128,2304]{1,0:T(8,128)(2,1)}) custom-call(f32[16,128]{1,0:T(8,128)} %get-tuple-element.201.refs_0_, f32[16,128]{1,0:T(8,128)} %copy-done.52, bf16[72,2304]{1,0:T(8,128)(2,1)} %get-tuple-element.133.refs_2_, bf16[72,2304]{1,0:T(8,128)(2,1)} %copy-done.10, bf16[72,2304]{1,0:T(8,128)(2,1)} %copy-done.11, ...), custom_call_target="tpu_custom_call" | custom-call | flops 679477248 | bytes 3833856 | tf_op jit(solution)/shard_map/pallas_call | solution.py:113
  373.6 2.8 collective-permute-start.94
  377.2 8.2 %shared.1.refs_0_ = f32[128,2304]{1,0:T(8,128)} custom-call(bf16[128,2304]{1,0:T(8,128)(2,1)} %refs_2_.8, bf16[128,2304]{1,0:T(8,128)(2,1)} %refs_2_.9, bf16[2304,128]{1,0:T(8,128)(2,1)} %refs_2_.5, bf16[2304,128]{1,0:T(8,128)(2,1)} %copy-done, bf16[2304,128]{1,0:T(8,128)(2,1)} %copy-done.3, bf16[2304,128]{1,0:T(8,128)(2,1)} %copy-done.6, ...), custom_call_target="tpu_custom_call" | custom-call | flops 1509949440 | bytes 7077888 | tf_op jit(solution)/shard_map/shared/pallas_call | solution.py:300
  387.8 5.7 %collective-permute-done.95.refs_7_ = bf16[128,768]{1,0:T(8,128)(2,1)S(1)} collective-permute-done((bf16[128,768]{1,0:T(8,128)(2,1)}, bf16[128,768]{1,0:T(8,128)(2,1)S(1)}, u32[]{:S(2)}, u32[]{:S(2)}) %collective-permute-start.95) | collective-permute-done | bytes 196640 | tf_op jit(solution)/shard_map/ppermute | solution.py:362
  393.5 2.8 collective-permute-done.77.refs_3_
  396.3 5.3 %collective-permute-done.94.refs_6_ = bf16[128,768]{1,0:T(8,128)(2,1)S(1)} collective-permute-done((bf16[128,768]{1,0:T(8,128)(2,1)}, bf16[128,768]{1,0:T(8,128)(2,1)S(1)}, u32[]{:S(2)}, u32[]{:S(2)}) %collective-permute-start.94) | collective-permute-done | bytes 196640 | tf_op jit(solution)/shard_map/ppermute | solution.py:362
  401.6 6.8 %collective-permute-done.49.refs_2_ = bf16[128,2304]{1,0:T(8,128)(2,1)S(1)} collective-permute-done((bf16[128,2304]{1,0:T(8,128)(2,1)}, bf16[128,2304]{1,0:T(8,128)(2,1)S(1)}, u32[]{:S(2)}, u32[]{:S(2)}) %collective-permute-start.49) | collective-permute-done | bytes 589856 | tf_op jit(solution)/shard_map/ppermute | solution.py:362
  409.3 3.2 finish.1
  (384 shorter events, 118.2 us)
Async XLA Ops:
  1.8 34.0 %collective-permute-start.10 = (bf16[128,768]{1,0:T(8,128)(2,1)S(1)}, bf16[128,768]{1,0:T(8,128)(2,1)S(1)}, u32[]{:S(2)}, u32[]{:S(2)}) collective-permute-start(bf16[128,768]{1,0:T(8,128)(2,1)S(1)} %get-tuple-element.199), channel_id=1, source_target_pairs={{0,16},{1,17},{2,18},{3,19},{4,20},{5,21},{6,22},{7,23},{8,24},{9,... | collective-permute-start | bytes 589832 | tf_op jit(solution)/shard_map/ppermute | solution.py:362
  5.9 34.6 %collective-permute-start.18 = (bf16[128,768]{1,0:T(8,128)(2,1)S(1)}, bf16[128,768]{1,0:T(8,128)(2,1)S(1)}, u32[]{:S(2)}, u32[]{:S(2)}) collective-permute-start(bf16[128,768]{1,0:T(8,128)(2,1)S(1)} %get-tuple-element.198), channel_id=1, source_target_pairs={{0,16},{1,17},{2,18},{3,19},{4,20},{5,21},{6,22},{7,23},{8,24},{9,... | collective-permute-start | bytes 589832 | tf_op jit(solution)/shard_map/ppermute | solution.py:362
  6.0 36.1 %collective-permute-start.26 = (bf16[128,768]{1,0:T(8,128)(2,1)S(1)}, bf16[128,768]{1,0:T(8,128)(2,1)S(1)}, u32[]{:S(2)}, u32[]{:S(2)}) collective-permute-start(bf16[128,768]{1,0:T(8,128)(2,1)S(1)} %get-tuple-element.197), channel_id=1, source_target_pairs={{0,16},{1,17},{2,18},{3,19},{4,20},{5,21},{6,22},{7,23},{8,24},{9,... | collective-permute-start | bytes 589832 | tf_op jit(solution)/shard_map/ppermute | solution.py:362
  11.3 27.4 %collective-permute-start.50 = (f32[16,128]{1,0:T(8,128)S(1)}, f32[16,128]{1,0:T(8,128)S(1)}, u32[]{:S(2)}, u32[]{:S(2)}) collective-permute-start(f32[16,128]{1,0:T(8,128)S(1)} %get-tuple-element.203), channel_id=1, source_target_pairs={{0,8},{1,9},{2,10},{3,11},{4,12},{5,13},{6,14},{7,15},{8,0},{9,1},... | collective-permute-start | bytes 24584 | tf_op jit(solution)/shard_map/ppermute | solution.py:362
  42.1 43.6 %collective-permute-start.52 = (bf16[128,2304]{1,0:T(8,128)(2,1)}, bf16[128,2304]{1,0:T(8,128)(2,1)S(1)}, u32[]{:S(2)}, u32[]{:S(2)}) collective-permute-start(bf16[128,2304]{1,0:T(8,128)(2,1)} %refs_2_.8), channel_id=1, source_target_pairs={{0,8},{1,9},{2,10},{3,11},{4,12},{5,13},{6,14},{7,15},{8,0},{9,1},... | collective-permute-start | bytes 1769480 | tf_op jit(solution)/shard_map/ppermute | solution.py:362
  82.1 27.8 %collective-permute-start.61 = (bf16[128,2304]{1,0:T(8,128)(2,1)}, bf16[128,2304]{1,0:T(8,128)(2,1)S(1)}, u32[]{:S(2)}, u32[]{:S(2)}) collective-permute-start(bf16[128,2304]{1,0:T(8,128)(2,1)} %refs_2_.9), channel_id=1, source_target_pairs={{0,8},{1,9},{2,10},{3,11},{4,12},{5,13},{6,14},{7,15},{8,0},{9,1},... | collective-permute-start | bytes 1769480 | tf_op jit(solution)/shard_map/ppermute | solution.py:362
  82.1 28.5 %collective-permute-start.62 = (bf16[128,2304]{1,0:T(8,128)(2,1)}, bf16[128,2304]{1,0:T(8,128)(2,1)S(1)}, u32[]{:S(2)}, u32[]{:S(2)}) collective-permute-start(bf16[128,2304]{1,0:T(8,128)(2,1)} %refs_2_.9), channel_id=1, source_target_pairs={{0,24},{1,25},{2,26},{3,27},{4,28},{5,29},{6,30},{7,31},{8,16},{9,... | collective-permute-start | bytes 1769480 | tf_op jit(solution)/shard_map/ppermute | solution.py:362
  83.6 59.7 %collective-permute-start.34 = (bf16[128,2304]{1,0:T(8,128)(2,1)}, bf16[128,2304]{1,0:T(8,128)(2,1)S(1)}, u32[]{:S(2)}, u32[]{:S(2)}) collective-permute-start(bf16[128,2304]{1,0:T(8,128)(2,1)} %refs_2_.9), channel_id=1, source_target_pairs={{0,16},{1,17},{2,18},{3,19},{4,20},{5,21},{6,22},{7,23},{8,24},{9,... | collective-permute-start | bytes 1769480 | tf_op jit(solution)/shard_map/ppermute | solution.py:362
  85.7 57.8 %collective-permute-start = (bf16[2304,128]{1,0:T(8,128)(2,1)}, bf16[2304,128]{1,0:T(8,128)(2,1)S(1)}, u32[]{:S(2)}, u32[]{:S(2)}) collective-permute-start(bf16[2304,128]{1,0:T(8,128)(2,1)} %refs_2_.5), channel_id=1, source_target_pairs={{0,2},{1,3},{2,0},{3,1},{4,6},{5,7},{6,4},{7,5},{8,10},{9,11},{10,... | collective-permute-start | bytes 1769480 | tf_op jit(solution)/shard_map/ppermute | solution.py:362
  85.8 62.4 %collective-permute-start.3 = (bf16[2304,128]{1,0:T(8,128)(2,1)}, bf16[2304,128]{1,0:T(8,128)(2,1)S(1)}, u32[]{:S(2)}, u32[]{:S(2)}) collective-permute-start(bf16[2304,128]{1,0:T(8,128)(2,1)} %refs_6_.1), channel_id=1, source_target_pairs={{0,2},{1,3},{2,0},{3,1},{4,6},{5,7},{6,4},{7,5},{8,10},{9,11},{10,... | collective-permute-start | bytes 1769480 | tf_op jit(solution)/shard_map/ppermute | solution.py:362
  110.0 38.4 %collective-permute-start.6 = (bf16[2304,128]{1,0:T(8,128)(2,1)}, bf16[2304,128]{1,0:T(8,128)(2,1)S(1)}, u32[]{:S(2)}, u32[]{:S(2)}) collective-permute-start(bf16[2304,128]{1,0:T(8,128)(2,1)} %refs_10_.1), channel_id=1, source_target_pairs={{0,2},{1,3},{2,0},{3,1},{4,6},{5,7},{6,4},{7,5},{8,10},{9,11},{10,... | collective-permute-start | bytes 1769480 | tf_op jit(solution)/shard_map/ppermute | solution.py:362
  110.7 39.1 %collective-permute-start.1 = (bf16[2304,128]{1,0:T(8,128)(2,1)}, bf16[2304,128]{1,0:T(8,128)(2,1)S(1)}, u32[]{:S(2)}, u32[]{:S(2)}) collective-permute-start(bf16[2304,128]{1,0:T(8,128)(2,1)} %refs_2_.5), channel_id=1, source_target_pairs={{0,1},{1,0},{2,3},{3,2},{4,5},{5,4},{6,7},{7,6},{8,9},{9,8},{10,11... | collective-permute-start | bytes 1769480 | tf_op jit(solution)/shard_map/ppermute | solution.py:362
  151.6 29.3 %collective-permute-start.58 = (bf16[72,2304]{1,0:T(8,128)(2,1)}, bf16[72,2304]{1,0:T(8,128)(2,1)S(1)}, u32[]{:S(2)}, u32[]{:S(2)}) collective-permute-start(bf16[72,2304]{1,0:T(8,128)(2,1)} %get-tuple-element.148), channel_id=1, source_target_pairs={{0,5},{1,4},{2,7},{3,6},{4,1},{5,0},{6,3},{7,2},{8,13},{9,12},{10,... | collective-permute-start | bytes 995336 | tf_op jit(solution)/shard_map/ppermute | solution.py:362
  151.9 31.0 %collective-permute-start.59 = (bf16[72,2304]{1,0:T(8,128)(2,1)}, bf16[72,2304]{1,0:T(8,128)(2,1)S(1)}, u32[]{:S(2)}, u32[]{:S(2)}) collective-permute-start(bf16[72,2304]{1,0:T(8,128)(2,1)} %get-tuple-element.149), channel_id=1, source_target_pairs={{0,6},{1,7},{2,4},{3,5},{4,2},{5,3},{6,0},{7,1},{8,14},{9,15},{10,... | collective-permute-start | bytes 995336 | tf_op jit(solution)/shard_map/ppermute | solution.py:362
  159.3 28.9 %collective-permute-start.60 = (bf16[72,2304]{1,0:T(8,128)(2,1)}, bf16[72,2304]{1,0:T(8,128)(2,1)S(1)}, u32[]{:S(2)}, u32[]{:S(2)}) collective-permute-start(bf16[72,2304]{1,0:T(8,128)(2,1)} %get-tuple-element.150), channel_id=1, source_target_pairs={{0,7},{1,6},{2,5},{3,4},{4,3},{5,2},{6,1},{7,0},{8,15},{9,14},{10,... | collective-permute-start | bytes 995336 | tf_op jit(solution)/shard_map/ppermute | solution.py:362
  212.8 32.9 %collective-permute-start.37 = (bf16[72,2304]{1,0:T(8,128)(2,1)}, bf16[72,2304]{1,0:T(8,128)(2,1)}, u32[]{:S(2)}, u32[]{:S(2)}) collective-permute-start(bf16[72,2304]{1,0:T(8,128)(2,1)} %get-tuple-element.128), channel_id=1, source_target_pairs={{0,3},{1,2},{2,1},{3,0},{4,7},{5,6},{6,5},{7,4},{8,11},{9,10},{10,... | collective-permute-start | bytes 995336 | tf_op jit(solution)/shard_map/ppermute | solution.py:362
  214.4 31.5 %collective-permute-start.38 = (bf16[72,2304]{1,0:T(8,128)(2,1)}, bf16[72,2304]{1,0:T(8,128)(2,1)}, u32[]{:S(2)}, u32[]{:S(2)}) collective-permute-start(bf16[72,2304]{1,0:T(8,128)(2,1)} %get-tuple-element.129), channel_id=1, source_target_pairs={{0,4},{1,5},{2,6},{3,7},{4,0},{5,1},{6,2},{7,3},{8,12},{9,13},{10,... | collective-permute-start | bytes 995336 | tf_op jit(solution)/shard_map/ppermute | solution.py:362
  215.8 31.3 %collective-permute-start.39 = (bf16[72,2304]{1,0:T(8,128)(2,1)}, bf16[72,2304]{1,0:T(8,128)(2,1)}, u32[]{:S(2)}, u32[]{:S(2)}) collective-permute-start(bf16[72,2304]{1,0:T(8,128)(2,1)} %get-tuple-element.130), channel_id=1, source_target_pairs={{0,5},{1,4},{2,7},{3,6},{4,1},{5,0},{6,3},{7,2},{8,13},{9,12},{10,... | collective-permute-start | bytes 995336 | tf_op jit(solution)/shard_map/ppermute | solution.py:362
  215.8 31.8 %collective-permute-start.40 = (bf16[72,2304]{1,0:T(8,128)(2,1)}, bf16[72,2304]{1,0:T(8,128)(2,1)}, u32[]{:S(2)}, u32[]{:S(2)}) collective-permute-start(bf16[72,2304]{1,0:T(8,128)(2,1)} %get-tuple-element.131), channel_id=1, source_target_pairs={{0,6},{1,7},{2,4},{3,5},{4,2},{5,3},{6,0},{7,1},{8,14},{9,15},{10,... | collective-permute-start | bytes 995336 | tf_op jit(solution)/shard_map/ppermute | solution.py:362
  217.2 31.9 %collective-permute-start.41 = (bf16[72,2304]{1,0:T(8,128)(2,1)}, bf16[72,2304]{1,0:T(8,128)(2,1)}, u32[]{:S(2)}, u32[]{:S(2)}) collective-permute-start(bf16[72,2304]{1,0:T(8,128)(2,1)} %get-tuple-element.132), channel_id=1, source_target_pairs={{0,7},{1,6},{2,5},{3,4},{4,3},{5,2},{6,1},{7,0},{8,15},{9,14},{10,... | collective-permute-start | bytes 995336 | tf_op jit(solution)/shard_map/ppermute | solution.py:362
  259.4 32.5 %collective-permute-start.80 = (bf16[72,768]{1,0:T(8,128)(2,1)}, bf16[72,768]{1,0:T(8,128)(2,1)S(1)}, u32[]{:S(2)}, u32[]{:S(2)}) collective-permute-start(bf16[72,768]{1,0:T(8,128)(2,1)} %get-tuple-element.171), channel_id=1, source_target_pairs={{0,3},{1,2},{2,1},{3,0},{4,7},{5,6},{6,5},{7,4},{8,11},{9,10},{10,... | collective-permute-start | bytes 331784 | tf_op jit(solution)/shard_map/ppermute | solution.py:362
  261.3 30.8 %collective-permute-start.81 = (bf16[72,768]{1,0:T(8,128)(2,1)}, bf16[72,768]{1,0:T(8,128)(2,1)S(1)}, u32[]{:S(2)}, u32[]{:S(2)}) collective-permute-start(bf16[72,768]{1,0:T(8,128)(2,1)} %get-tuple-element.172), channel_id=1, source_target_pairs={{0,4},{1,5},{2,6},{3,7},{4,0},{5,1},{6,2},{7,3},{8,12},{9,13},{10,... | collective-permute-start | bytes 331784 | tf_op jit(solution)/shard_map/ppermute | solution.py:362
  262.7 30.2 %collective-permute-start.82 = (bf16[72,768]{1,0:T(8,128)(2,1)}, bf16[72,768]{1,0:T(8,128)(2,1)S(1)}, u32[]{:S(2)}, u32[]{:S(2)}) collective-permute-start(bf16[72,768]{1,0:T(8,128)(2,1)} %get-tuple-element.173), channel_id=1, source_target_pairs={{0,5},{1,4},{2,7},{3,6},{4,1},{5,0},{6,3},{7,2},{8,13},{9,12},{10,... | collective-permute-start | bytes 331784 | tf_op jit(solution)/shard_map/ppermute | solution.py:362
  262.7 31.1 %collective-permute-start.83 = (bf16[72,768]{1,0:T(8,128)(2,1)}, bf16[72,768]{1,0:T(8,128)(2,1)S(1)}, u32[]{:S(2)}, u32[]{:S(2)}) collective-permute-start(bf16[72,768]{1,0:T(8,128)(2,1)} %get-tuple-element.174), channel_id=1, source_target_pairs={{0,6},{1,7},{2,4},{3,5},{4,2},{5,3},{6,0},{7,1},{8,14},{9,15},{10,... | collective-permute-start | bytes 331784 | tf_op jit(solution)/shard_map/ppermute | solution.py:362
  264.0 30.2 %collective-permute-start.84 = (bf16[72,768]{1,0:T(8,128)(2,1)}, bf16[72,768]{1,0:T(8,128)(2,1)S(1)}, u32[]{:S(2)}, u32[]{:S(2)}) collective-permute-start(bf16[72,768]{1,0:T(8,128)(2,1)} %get-tuple-element.175), channel_id=1, source_target_pairs={{0,7},{1,6},{2,5},{3,4},{4,3},{5,2},{6,1},{7,0},{8,15},{9,14},{10,... | collective-permute-start | bytes 331784 | tf_op jit(solution)/shard_map/ppermute | solution.py:362
  292.9 27.3 %collective-permute-start.44 = (bf16[72,2304]{1,0:T(8,128)(2,1)}, bf16[72,2304]{1,0:T(8,128)(2,1)S(1)}, u32[]{:S(2)}, u32[]{:S(2)}) collective-permute-start(bf16[72,2304]{1,0:T(8,128)(2,1)} %get-tuple-element.136), channel_id=1, source_target_pairs={{0,3},{1,2},{2,1},{3,0},{4,7},{5,6},{6,5},{7,4},{8,11},{9,10},{10,... | collective-permute-start | bytes 995336 | tf_op jit(solution)/shard_map/ppermute | solution.py:362
  295.4 66.8 %collective-permute-start.2 = (bf16[2304,128]{1,0:T(8,128)(2,1)S(1)}, bf16[2304,128]{1,0:T(8,128)(2,1)S(1)}, u32[]{:S(2)}, u32[]{:S(2)}) collective-permute-start(bf16[2304,128]{1,0:T(8,128)(2,1)S(1)} %collective-permute-done.refs_3_), channel_id=1, source_target_pairs={{0,1},{1,0},{2,3},{3,2},{4,5},{5,4},{6,7},{7,6},{8,9},{9,8},{10,11... | collective-permute-start | bytes 1769480 | tf_op jit(solution)/shard_map/ppermute | solution.py:362
  318.6 29.8 %collective-permute-start.46 = (bf16[72,2304]{1,0:T(8,128)(2,1)}, bf16[72,2304]{1,0:T(8,128)(2,1)S(1)}, u32[]{:S(2)}, u32[]{:S(2)}) collective-permute-start(bf16[72,2304]{1,0:T(8,128)(2,1)} %get-tuple-element.138), channel_id=1, source_target_pairs={{0,5},{1,4},{2,7},{3,6},{4,1},{5,0},{6,3},{7,2},{8,13},{9,12},{10,... | collective-permute-start | bytes 995336 | tf_op jit(solution)/shard_map/ppermute | solution.py:362
  318.6 31.6 %collective-permute-start.47 = (bf16[72,2304]{1,0:T(8,128)(2,1)}, bf16[72,2304]{1,0:T(8,128)(2,1)S(1)}, u32[]{:S(2)}, u32[]{:S(2)}) collective-permute-start(bf16[72,2304]{1,0:T(8,128)(2,1)} %get-tuple-element.139), channel_id=1, source_target_pairs={{0,6},{1,7},{2,4},{3,5},{4,2},{5,3},{6,0},{7,1},{8,14},{9,15},{10,... | collective-permute-start | bytes 995336 | tf_op jit(solution)/shard_map/ppermute | solution.py:362
  320.2 31.0 %collective-permute-start.48 = (bf16[72,2304]{1,0:T(8,128)(2,1)}, bf16[72,2304]{1,0:T(8,128)(2,1)S(1)}, u32[]{:S(2)}, u32[]{:S(2)}) collective-permute-start(bf16[72,2304]{1,0:T(8,128)(2,1)} %get-tuple-element.140), channel_id=1, source_target_pairs={{0,7},{1,6},{2,5},{3,4},{4,3},{5,2},{6,1},{7,0},{8,15},{9,14},{10,... | collective-permute-start | bytes 995336 | tf_op jit(solution)/shard_map/ppermute | solution.py:362
  362.2 46.2 %collective-permute-start.49 = (bf16[128,2304]{1,0:T(8,128)(2,1)}, bf16[128,2304]{1,0:T(8,128)(2,1)S(1)}, u32[]{:S(2)}, u32[]{:S(2)}) collective-permute-start(bf16[128,2304]{1,0:T(8,128)(2,1)} %get-tuple-element.142), channel_id=1, source_target_pairs={{0,16},{1,17},{2,18},{3,19},{4,20},{5,21},{6,22},{7,23},{8,24},{9,... | collective-permute-start | bytes 1769480 | tf_op jit(solution)/shard_map/ppermute | solution.py:362
  373.6 28.0 %collective-permute-start.94 = (bf16[128,768]{1,0:T(8,128)(2,1)}, bf16[128,768]{1,0:T(8,128)(2,1)S(1)}, u32[]{:S(2)}, u32[]{:S(2)}) collective-permute-start(bf16[128,768]{1,0:T(8,128)(2,1)} %get-tuple-element.186), channel_id=1, source_target_pairs={{0,24},{1,25},{2,26},{3,27},{4,28},{5,29},{6,30},{7,31},{8,16},{9,... | collective-permute-start | bytes 589832 | tf_op jit(solution)/shard_map/ppermute | solution.py:362
  (165 other events, 5698.9 us)

commit v2 on v1

--- a/solution.py
+++ b/solution.py
@@ -54,34 +54,51 @@
 
 
 def tile_of(width):
-    return 768 if width % 768 == 0 else width
-
-
-def pack_kernel(peers, cap, count, scaled, *refs):
-    info_refs, block_refs, out_refs = refs[:count], refs[count : 2 * count], refs[2 * count :]
+    return next((tile for tile in (768, 1152) if width % tile == 0), width)
+
+
+def pack_kernel(peers, cap, counts, scaled, *refs):
+    count = len(counts)
+    info_refs, block_refs, out_refs = refs[:count], list(refs[count:-peers]), refs[-peers:]
+    step = pl.program_id(0)
     hot, scale = selection(info_refs, peers, cap, scaled)
-    rows = jnp.concatenate([ref[...] for ref in block_refs], axis=0)
-    picked = dot(hot.astype(BF16), rows, 1, 0)
+    blocks = []
+    for n in counts:
+        pieces = [block_refs.pop(0)[...] for _ in range(n)]
+        block = pieces[0]
+        for c in range(1, n):
+            block = jnp.where(step == c, pieces[c], block)
+        blocks.append(block)
+    picked = dot(hot.astype(BF16), jnp.concatenate(blocks, axis=0), 1, 0)
     if scaled:
         picked = picked * scale
     for d in range(peers):
         out_refs[d][...] = picked[d * count * cap : (d + 1) * count * cap].astype(BF16)
 
 
-def pack(infos, blocks, peers, cap, scaled):
+def pack(infos, blocks, width, peers, cap, scaled):
     count = len(infos)
     tokens = infos[0].shape[1]
-    width = min(array.shape[1] for array, _ in blocks)
-    tile = tile_of(width)
+    cut = [block for block in blocks if isinstance(block, list) and len(block) > 1]
+    tile = cut[0][0].shape[1] if cut else tile_of(width)
     whole = pl.BlockSpec(infos[0].shape, lambda i: (0, 0))
-    parts = [
-        pl.BlockSpec((tokens, tile), functools.partial(lambda at, i: (0, i + at), start // tile))
-        for _, start in blocks
-    ]
+    arrays, specs, counts = [], [], []
+    for block in blocks:
+        if isinstance(block, list) and len(block) > 1:
+            arrays += block
+            specs += [pl.BlockSpec((tokens, tile), lambda i: (0, 0))] * len(block)
+            counts.append(len(block))
+            continue
+        array, start = block if isinstance(block, tuple) else (block[0], 0)
+        arrays.append(array)
+        specs.append(
+            pl.BlockSpec((tokens, tile), functools.partial(lambda at, i: (0, i + at), start // tile))
+        )
+        counts.append(1)
     return pl.pallas_call(
-        functools.partial(pack_kernel, peers, cap, count, scaled),
+        functools.partial(pack_kernel, peers, cap, tuple(counts), scaled),
         grid=(width // tile,),
-        in_specs=[whole] * count + parts,
+        in_specs=[whole] * count + specs,
         out_specs=[pl.BlockSpec((count * cap, tile), lambda i: (0, i))] * peers,
         out_shape=[jax.ShapeDtypeStruct((count * cap, width), BF16)] * peers,
         compiler_params=params(),
@@ -90,7 +107,7 @@
             bytes_accessed=2 * width * (peers * count * cap + count * tokens),
             transcendentals=0,
         ),
-    )(*infos, *[array for array, _ in blocks])
+    )(*infos, *arrays)
 
 
 def merge_kernel(peers, cap, count, *refs):
@@ -276,30 +293,47 @@
     )(base, *flat)
 
 
-def shared_kernel(slices, *refs):
-    rows, grads = refs[0], refs[1]
-    gates, ups, downs = (refs[2 + i * slices : 2 + (i + 1) * slices] for i in range(3))
-    out = refs[2 + 3 * slices]
-    for i in range(slices):
-        gate_w, up_w = gates[i][...], ups[i][...]
+def shared_kernel(full, parts, quarters, *refs):
+    place, rows, grads = refs[:3]
+    refs = refs[3:]
+    width = rows.shape[1]
+    out, stack_ref = refs[-2:]
+
+    def add(stack, first):
+        gate_w, up_w = stack[:width], stack[width : 2 * width]
         gate_pre = dot(rows[...], gate_w, 1, 0)
         up_pre = dot(rows[...], up_w, 1, 0)
-        d_hidden = dot(grads[...], downs[i][...], 1, 0)
+        d_hidden = dot(grads[...], stack[2 * width :], 1, 0)
         d_gate, d_up = cotangents(gate_pre, up_pre, d_hidden)
         part = dot(d_gate, gate_w, 1, 1) + dot(d_up, up_w, 1, 1)
-        if i == 0:
+        if first:
             out[...] = part
         else:
             out[...] += part
 
-
-def shared(rows, grads, gates, ups, downs):
-    slices = len(gates)
-    hidden = gates[0].shape[1]
+    for i in range(full):
+        add(refs[i], i == 0)
+    for i in range(parts):
+        for j in range(quarters):
+            piece = refs[full + i * quarters + j]
+            size = piece.shape[0]
+            at = pl.multiple_of(jnp.bitwise_xor(place[0], j) * size, size)
+            stack_ref[pl.ds(at, size), :] = piece[...]
+        add(stack_ref, False)
+
+
+def shared(place, rows, grads, whole_stacks, cut_stacks):
+    full, parts, quarters = len(whole_stacks), len(cut_stacks), len(cut_stacks[0])
+    tall, hidden = whole_stacks[0].shape
     count, width = rows.shape
+    slices = full + parts
+    vmem = pl.BlockSpec(memory_space=pltpu.VMEM)
+    flat = whole_stacks + [piece for stack in cut_stacks for piece in stack]
     return pl.pallas_call(
-        functools.partial(shared_kernel, slices),
+        functools.partial(shared_kernel, full, parts, quarters),
+        in_specs=[pl.BlockSpec(memory_space=pltpu.SMEM)] + [vmem] * (2 + len(flat)),
         out_shape=jax.ShapeDtypeStruct((count, width), F32),
+        scratch_shapes=[pltpu.VMEM((tall, hidden), BF16)],
         compiler_params=params(),
         cost_estimate=pl.CostEstimate(
             flops=10 * count * width * hidden * slices,
@@ -307,7 +341,7 @@
             transcendentals=count * hidden * slices,
         ),
         name="shared",
-    )(rows, grads, *gates, *ups, *downs)
+    )(place, rows, grads, *flat)
 
 
 def halvings(count):
@@ -323,11 +357,11 @@
 
 
 def widths(width, pieces):
-    return [width // pieces] * pieces if width % (768 * pieces) == 0 else [width]
-
-
-IN_PIECES = 3
-OUT_PIECES = 3
+    return [width // pieces] * pieces if width % (128 * pieces) == 0 else [width]
+
+
+IN_PIECES = 2
+OUT_PIECES = 2
 
 
 def local(
@@ -390,35 +424,55 @@
         up_adapter_in[0],
         up_adapter_out[0],
     )
-    slices = {"gate": [shared_gate], "up": [shared_up], "down": [shared_down]}
-    for bit in halvings(rep_count):
-        for kind, held in slices.items():
-            slices[kind] = held + [swap(piece, 0, bit) for piece in held]
-
-    def pieces(array, p, sizes):
-        if p == 0:
-            return [(array, sum(sizes[:c])) for c in range(len(sizes))]
-        found = []
-        for c, size in enumerate(sizes):
-            start = sum(sizes[:c])
-            found.append((swap(array[:, start : start + size], p, 0), 0))
-        return found
+    far, *rest = halvings(rep_count)
+    place = (me // rep_count) % 4
+    stack = jnp.concatenate([shared_gate, shared_up, shared_down], axis=0)
+    quarter = stack.shape[0] // 4
+    cut = [swap(lax.dynamic_slice_in_dim(stack, place * quarter, quarter), 0, far)]
+    cut = cut + [swap(cut[0], 0, rep_count)]
+    cut = cut + [swap(piece, 1, 0) for piece in cut]
+    whole_stacks, cut_stacks = [stack], [cut]
+    for bit in rest:
+        whole_stacks = whole_stacks + [swap(s, 0, bit) for s in whole_stacks]
+        cut_stacks = cut_stacks + [
+            [swap(piece, 0, bit) for piece in pieces]
+            for pieces in cut_stacks
+        ]
+
+    def blocks_of(array, sizes):
+        held = {1: [swap(array, 1, 0)]}
+        for p in groups[0]:
+            pieces = []
+            for c, size in enumerate(sizes):
+                start = sum(sizes[:c])
+                if p == 0:
+                    pieces.append((array, start))
+                    continue
+                piece = array if len(sizes) == 1 else array[:, start : start + size]
+                pieces.append(swap(piece, p, 0))
+                held.setdefault(p + 1, []).append(swap(pieces[-1], 1, 0))
+            held[p] = pieces
+        return held
 
     def fan_out(arrays):
         return [swap(arrays[d], 0, d) for d in range(peers)]
 
+    token_blocks = blocks_of(tokens, in_widths)
+    grad_blocks = blocks_of(output_grad, every)
     terms = []
     adapter = []
     for g, group in enumerate(groups):
         seen = [infos[p] for p in group]
         sizes, out_sizes = (in_widths, every) if g == 0 else (every, out_widths)
-        blocks = [pieces(tokens, p, sizes) for p in group]
         rows = []
-        for c in range(len(sizes)):
-            packed = pack(seen, [block[c] for block in blocks], peers, cap, False)
+        for c, size in enumerate(sizes):
+            blocks = [token_blocks[p] if g else token_blocks[p][c] for p in group]
+            blocks = [b if isinstance(b, (list, tuple)) else (b, 0) for b in blocks]
+            packed = pack(seen, blocks, size, peers, cap, False)
             rows.append(fan_out(packed))
-        blocks = [pieces(output_grad, p, every) for p in group]
-        packed = pack(seen, [block[0] for block in blocks], peers, cap, True)
+        blocks = [grad_blocks[p] if g else grad_blocks[p][0] for p in group]
+        blocks = [b if isinstance(b, (list, tuple)) else (b, 0) for b in blocks]
+        packed = pack(seen, blocks, model_width, peers, cap, True)
         grads = [fan_out(packed)]
         outs, grads_of_maps = expert(rows, grads, weights, out_sizes)
         adapter.append(grads_of_maps)
@@ -430,7 +484,7 @@
             for p, part in zip(group, merged):
                 found[p].append(swap(part, p, 0))
         terms += list(found.values())
-    base = shared(tokens, output_grad, *slices.values())
+    base = shared(place.reshape(1), tokens, output_grad, whole_stacks, cut_stacks)
     token_grad = finish(base, terms)
     adapter_grads = [sum(pieces[1:], pieces[0])[None] for pieces in zip(*adapter)]
     return (token_grad, *adapter_grads)

time: 418 us -> 383 us (0.916)
  waiting for transfers between devices: 204 us -> 186 us
  starting transfers between devices: 103 us -> 88.2 us
  local copies, waits for them, and re-layouts: 3.01 us -> 8.78 us
    ppermute x97 -> x81, waiting for transfers between devices: 204 us -> 186 us  [swap(): return lax.ppermute(array, AXES, [(i, i ^ step) for i in range(owners)])]
    ppermute x97 -> x81, starting transfers between devices: 103 us -> 88.2 us  [swap(): return lax.ppermute(array, AXES, [(i, i ^ step) for i in range(owners)])]
    unnamed x200 -> x172, local copies, waits for them, and re-layouts: 1.84 us -> 7.47 us
    pallas_call x7 -> x6, Pallas kernels: 27.2 us -> 25.2 us  [the longest x5 17 us: pack(): pl.pallas_call(functools.partial(pack_kernel, peers, cap, tuple(counts),...]
    pallas_call x4 -> x3, Pallas kernels: 12.4 us -> 10.5 us  [merge(): pl.pallas_call(functools.partial(merge_kernel, peers, cap, count), grid=(...]
  transfers between devices with their start and end apart: 97 -> 81, of which waited for: 29 -> 27; matrix products, arithmetic and copies ran while one was open for 1% -> 1% of each run, Pallas kernels for 22% -> 23%
where the time goes in v2:
time: 383 us; the launch traced here: 380 us
  waiting for transfers between devices  186 us (49%)
  Pallas kernels  91.8 us (24%)
  starting transfers between devices  88.2 us (23%)
  local copies, waits for them, and re-layouts  8.78 us (2%)
  other arithmetic  4.1 us (1%)
    ppermute x81, waiting for transfers between devices, swap(): return lax.ppermute(array, AXES, [(i, i ^ step) for i in range(owners)])  186 us
    ppermute x81, starting transfers between devices, swap(): return lax.ppermute(array, AXES, [(i, i ^ step) for i in range(owners)])  88.2 us
    pallas_call x2, Pallas kernels, expert(): pl.pallas_call(functools.partial(expert_kernel, peers, steps, (len(rows),...  52.9 us
    pallas_call x5, Pallas kernels, pack(): pl.pallas_call(functools.partial(pack_kernel, peers, cap, tuple(counts),...  17 us
    pallas_call x3, Pallas kernels, merge(): pl.pallas_call(functools.partial(merge_kernel, peers, cap, count), grid=(...  10.5 us
    pallas_call x1, Pallas kernels, shared(): pl.pallas_call(functools.partial(shared_kernel, full, parts, quarters), i...  8.22 us
  transfers between devices with their start and end apart: 81, of which 27 were waited for; matrix products, arithmetic and copies ran while one was open for 1% of the time, Pallas kernels for 23%

profile of v2, /device:TPU:0, one launch (start us, length us, event | category | flops | bytes accessed | tf_op | source)
XLA Modules:
  0.0 380.3 jit_solution(14352580415243464134)
XLA Ops:
  1.8 4.1 %collective-permute-start.10 = (bf16[128,1152]{1,0:T(8,128)(2,1)S(1)}, bf16[128,1152]{1,0:T(8,128)(2,1)}, u32[]{:S(2)}, u32[]{:S(2)}) collective-permute-start(bf16[128,1152]{1,0:T(8,128)(2,1)S(1)} %get-tuple-element.162), channel_id=1, source_target_pairs={{0,16},{1,17},{2,18},{3,19},{4,20},{5,21},{6,22},{7,23},{8,24},{9,... | collective-permute-start | bytes 884744 | tf_op jit(solution)/shard_map/ppermute | solution.py:396
  12.9 19.4 %collective-permute-done.9.refs_1_ = f32[16,128]{1,0:T(8,128)S(1)} collective-permute-done((f32[16,128]{1,0:T(8,128)S(1)}, f32[16,128]{1,0:T(8,128)S(1)}, u32[]{:S(2)}, u32[]{:S(2)}) %collective-permute-start.9) | collective-permute-done | bytes 8224 | tf_op jit(solution)/shard_map/ppermute | solution.py:396
  40.7 3.6 collective-permute-start.43
  53.8 6.9 %collective-permute-done.14.refs_4_ = bf16[72,1152]{1,0:T(8,128)(2,1)S(1)} collective-permute-done((bf16[72,1152]{1,0:T(8,128)(2,1)}, bf16[72,1152]{1,0:T(8,128)(2,1)S(1)}, u32[]{:S(2)}, u32[]{:S(2)}) %collective-permute-start.14) | collective-permute-done | bytes 165920 | tf_op jit(solution)/shard_map/ppermute | solution.py:396
  65.5 3.8 %collective-permute-start.44 = (bf16[128,2304]{1,0:T(8,128)(2,1)S(1)}, bf16[128,2304]{1,0:T(8,128)(2,1)S(1)}, u32[]{:S(2)}, u32[]{:S(2)}) collective-permute-start(bf16[128,2304]{1,0:T(8,128)(2,1)S(1)} %copy-done.1), channel_id=1, source_target_pairs={{0,8},{1,9},{2,10},{3,11},{4,12},{5,13},{6,14},{7,15},{8,0},{9,1},... | collective-permute-start | bytes 1769480 | tf_op jit(solution)/shard_map/ppermute | solution.py:396
  72.9 9.5 %collective-permute-done.23.refs_13_ = bf16[72,1152]{1,0:T(8,128)(2,1)S(1)} collective-permute-done((bf16[72,1152]{1,0:T(8,128)(2,1)}, bf16[72,1152]{1,0:T(8,128)(2,1)S(1)}, u32[]{:S(2)}, u32[]{:S(2)}) %collective-permute-start.23) | collective-permute-done | bytes 165920 | tf_op jit(solution)/shard_map/ppermute | solution.py:396
  82.3 3.4 collective-permute-start.45
  87.9 13.3 %collective-permute-done.45.refs_3_ = bf16[128,1152]{1,0:T(8,128)(2,1)S(1)} collective-permute-done((bf16[128,1152]{1,0:T(8,128)(2,1)}, bf16[128,1152]{1,0:T(8,128)(2,1)S(1)}, u32[]{:S(2)}, u32[]{:S(2)}) %collective-permute-start.45) | collective-permute-done | bytes 294944 | tf_op jit(solution)/shard_map/ppermute | solution.py:396
  102.5 4.2 %shard_map.175 = (bf16[72,2304]{1,0:T(8,128)(2,1)}, bf16[72,2304]{1,0:T(8,128)(2,1)}, bf16[72,2304]{1,0:T(8,128)(2,1)}, bf16[72,2304]{1,0:T(8,128)(2,1)}, bf16[7...) custom-call(f32[16,128]{1,0:T(8,128)} %get-tuple-element.164.refs_0_, ...), custom_call_target="tpu_custom_call" | custom-call | flops 679477248 | bytes 3833856 | tf_op jit(solution)/shard_map/pallas_call | solution.py:98
  109.2 10.8 %collective-permute-done.54.refs_2_ = bf16[128,2304]{1,0:T(8,128)(2,1)S(1)} collective-permute-done((bf16[128,2304]{1,0:T(8,128)(2,1)S(1)}, bf16[128,2304]{1,0:T(8,128)(2,1)S(1)}, u32[]{:S(2)}, u32[]{:S(2)}) %collective-permute-start.54) | collective-permute-done | bytes 589856 | tf_op jit(solution)/shard_map/ppermute | solution.py:396
  121.3 8.3 %collective-permute-done.3.refs_7_ = bf16[1728,128]{1,0:T(8,128)(2,1)S(1)} collective-permute-done((bf16[1728,128]{1,0:T(8,128)(2,1)S(1)}, bf16[1728,128]{1,0:T(8,128)(2,1)S(1)}, u32[]{:S(2)}, u32[]{:S(2)}) %collective-permute-start.3) | collective-permute-done | bytes 442400 | tf_op jit(solution)/shard_map/ppermute | solution.py:396
  132.5 3.4 shard_map.178
  136.8 16.7 %collective-permute-done.31.refs_21_ = bf16[72,2304]{1,0:T(8,128)(2,1)S(1)} collective-permute-done((bf16[72,2304]{1,0:T(8,128)(2,1)}, bf16[72,2304]{1,0:T(8,128)(2,1)S(1)}, u32[]{:S(2)}, u32[]{:S(2)}) %collective-permute-start.31) | collective-permute-done | bytes 331808 | tf_op jit(solution)/shard_map/ppermute | solution.py:396
  156.1 26.4 %shard_map.176 = (bf16[72,2304]{1,0:T(8,128)(2,1)}, bf16[72,2304]{1,0:T(8,128)(2,1)}, bf16[72,2304]{1,0:T(8,128)(2,1)}, bf16[72,2304]{1,0:T(8,128)(2,1)}, bf16[7...) custom-call(bf16[72,1152]{1,0:T(8,128)(2,1)} %get-tuple-element.83.r, ...), custom_call_target="tpu_custom_call" | custom-call | flops 13589544960 | bytes 22118400 | tf_op jit(solution)/shard_map/pallas_call | solution.py:230
  187.3 4.1 %shard_map.179 = (bf16[72,2304]{1,0:T(8,128)(2,1)}, bf16[72,2304]{1,0:T(8,128)(2,1)}, bf16[72,2304]{1,0:T(8,128)(2,1)}, bf16[72,2304]{1,0:T(8,128)(2,1)}, bf16[7...) custom-call(f32[16,128]{1,0:T(8,128)} %copy-done.40, ...), custom_call_target="tpu_custom_call" | custom-call | flops 679477248 | bytes 3833856 | tf_op jit(solution)/shard_map/pallas_call | solution.py:98
  191.5 16.2 %collective-permute-done.50.refs_4_ = bf16[72,2304]{1,0:T(8,128)(2,1)S(1)} collective-permute-done((bf16[72,2304]{1,0:T(8,128)(2,1)}, bf16[72,2304]{1,0:T(8,128)(2,1)S(1)}, u32[]{:S(2)}, u32[]{:S(2)}) %collective-permute-start.50) | collective-permute-done | bytes 331808 | tf_op jit(solution)/shard_map/ppermute | solution.py:396
  209.7 3.9 %collective-permute-done.51.refs_5_ = bf16[72,2304]{1,0:T(8,128)(2,1)S(1)} collective-permute-done((bf16[72,2304]{1,0:T(8,128)(2,1)}, bf16[72,2304]{1,0:T(8,128)(2,1)S(1)}, u32[]{:S(2)}, u32[]{:S(2)}) %collective-permute-start.51) | collective-permute-done | bytes 331808 | tf_op jit(solution)/shard_map/ppermute | solution.py:396
  219.7 4.9 %collective-permute-done.36.refs_5_ = bf16[72,2304]{1,0:T(8,128)(2,1)S(1)} collective-permute-done((bf16[72,2304]{1,0:T(8,128)(2,1)S(1)}, bf16[72,2304]{1,0:T(8,128)(2,1)S(1)}, u32[]{:S(2)}, u32[]{:S(2)}) %collective-permute-start.36) | collective-permute-done | bytes 331808 | tf_op jit(solution)/shard_map/ppermute | solution.py:396
  228.6 3.8 %collective-permute-done.57.refs_10_ = bf16[72,2304]{1,0:T(8,128)(2,1)S(1)} collective-permute-done((bf16[72,2304]{1,0:T(8,128)(2,1)}, bf16[72,2304]{1,0:T(8,128)(2,1)S(1)}, u32[]{:S(2)}, u32[]{:S(2)}) %collective-permute-start.57) | collective-permute-done | bytes 331808 | tf_op jit(solution)/shard_map/ppermute | solution.py:396
  232.8 6.0 %collective-permute-done.58.refs_11_ = bf16[72,2304]{1,0:T(8,128)(2,1)S(1)} collective-permute-done((bf16[72,2304]{1,0:T(8,128)(2,1)}, bf16[72,2304]{1,0:T(8,128)(2,1)S(1)}, u32[]{:S(2)}, u32[]{:S(2)}) %collective-permute-start.58) | collective-permute-done | bytes 331808 | tf_op jit(solution)/shard_map/ppermute | solution.py:396
  241.0 15.6 %collective-permute-done.60.refs_13_ = bf16[72,2304]{1,0:T(8,128)(2,1)S(1)} collective-permute-done((bf16[72,2304]{1,0:T(8,128)(2,1)}, bf16[72,2304]{1,0:T(8,128)(2,1)S(1)}, u32[]{:S(2)}, u32[]{:S(2)}) %collective-permute-start.60) | collective-permute-done | bytes 331808 | tf_op jit(solution)/shard_map/ppermute | solution.py:396
  260.3 26.5 %shard_map.180 = (bf16[72,1152]{1,0:T(8,128)(2,1)}, bf16[72,1152]{1,0:T(8,128)(2,1)}, bf16[72,1152]{1,0:T(8,128)(2,1)}, bf16[72,1152]{1,0:T(8,128)(2,1)}, bf16[7...) custom-call(bf16[72,2304]{1,0:T(8,128)(2,1)} %get-tuple-element.117., ...), custom_call_target="tpu_custom_call" | custom-call | flops 13589544960 | bytes 22118400 | tf_op jit(solution)/shard_map/pallas_call | solution.py:230
  290.6 3.8 %collective-permute-done.72.refs_4_ = bf16[72,1152]{1,0:T(8,128)(2,1)S(1)} collective-permute-done((bf16[72,1152]{1,0:T(8,128)(2,1)}, bf16[72,1152]{1,0:T(8,128)(2,1)S(1)}, u32[]{:S(2)}, u32[]{:S(2)}) %collective-permute-start.72) | collective-permute-done | bytes 165920 | tf_op jit(solution)/shard_map/ppermute | solution.py:396
  299.9 5.8 %collective-permute-done.75.refs_7_ = bf16[72,1152]{1,0:T(8,128)(2,1)S(1)} collective-permute-done((bf16[72,1152]{1,0:T(8,128)(2,1)}, bf16[72,1152]{1,0:T(8,128)(2,1)S(1)}, u32[]{:S(2)}, u32[]{:S(2)}) %collective-permute-start.75) | collective-permute-done | bytes 165920 | tf_op jit(solution)/shard_map/ppermute | solution.py:396
  309.3 3.8 %collective-permute-done.64.refs_4_ = bf16[72,1152]{1,0:T(8,128)(2,1)S(1)} collective-permute-done((bf16[72,1152]{1,0:T(8,128)(2,1)}, bf16[72,1152]{1,0:T(8,128)(2,1)S(1)}, u32[]{:S(2)}, u32[]{:S(2)}) %collective-permute-start.64) | collective-permute-done | bytes 165920 | tf_op jit(solution)/shard_map/ppermute | solution.py:396
  315.4 3.3 collective-permute-start.69
  318.7 4.5 %shard_map.177 = (f32[128,2304]{1,0:T(8,128)}, bf16[128,2304]{1,0:T(8,128)(2,1)}) custom-call(f32[16,128]{1,0:T(8,128)} %get-tuple-element.164.refs_0_, f32[16,128]{1,0:T(8,128)} %copy-done.43, bf16[72,2304]{1,0:T(8,128)(2,1)} %get-tuple-element.107.refs_2_, bf16[72,2304]{1,0:T(8,128)(2,1)} %copy-done.15, bf16[72,2304]{1,0:T(8,128)(2,1)} %copy-done.16, ...), custom_call_target="tpu_custom_call" | custom-call | flops 679477248 | bytes 3833856 | tf_op jit(solution)/shard_map/pallas_call | solution.py:130
  342.4 8.2 %shared.1.refs_0_ = f32[128,2304]{1,0:T(8,128)} custom-call(s32[1]{0:T(128)} %bitcast.refs_0_, bf16[128,2304]{1,0:T(8,128)(2,1)} %refs_2_.6, bf16[128,2304]{1,0:T(8,128)(2,1)} %refs_2_.7, bf16[6912,128]{1,0:T(8,128)(2,1)} %copy-done, bf16[6912,128]{1,0:T(8,128)(2,1)} %copy-done.2, bf16[1728,128]{1,0:T(8,128)(2,1)} %copy-done.7, ...), custom_call_target="tpu_custom_call" | custom-call | flops 1509949440 | bytes 7077888 | tf_op jit(solution)/shard_map/shared/pallas_call | solution.py:332
  350.6 12.1 %collective-permute-done.41.refs_2_ = bf16[128,2304]{1,0:T(8,128)(2,1)S(1)} collective-permute-done((bf16[128,2304]{1,0:T(8,128)(2,1)}, bf16[128,2304]{1,0:T(8,128)(2,1)S(1)}, u32[]{:S(2)}, u32[]{:S(2)}) %collective-permute-start.41) | collective-permute-done | bytes 589856 | tf_op jit(solution)/shard_map/ppermute | solution.py:396
  362.7 7.7 %collective-permute-done.78.refs_4_ = bf16[128,1152]{1,0:T(8,128)(2,1)S(1)} collective-permute-done((bf16[128,1152]{1,0:T(8,128)(2,1)}, bf16[128,1152]{1,0:T(8,128)(2,1)S(1)}, u32[]{:S(2)}, u32[]{:S(2)}) %collective-permute-start.78) | collective-permute-done | bytes 294944 | tf_op jit(solution)/shard_map/ppermute | solution.py:396
  370.4 5.8 %collective-permute-done.70.refs_3_ = bf16[128,1152]{1,0:T(8,128)(2,1)S(1)} collective-permute-done((bf16[128,1152]{1,0:T(8,128)(2,1)}, bf16[128,1152]{1,0:T(8,128)(2,1)S(1)}, u32[]{:S(2)}, u32[]{:S(2)}) %collective-permute-start.70) | collective-permute-done | bytes 294944 | tf_op jit(solution)/shard_map/ppermute | solution.py:396
  377.1 3.2 finish.1
  (324 shorter events, 105.6 us)
Async XLA Ops:
  1.8 30.5 %collective-permute-start.10 = (bf16[128,1152]{1,0:T(8,128)(2,1)S(1)}, bf16[128,1152]{1,0:T(8,128)(2,1)}, u32[]{:S(2)}, u32[]{:S(2)}) collective-permute-start(bf16[128,1152]{1,0:T(8,128)(2,1)S(1)} %get-tuple-element.162), channel_id=1, source_target_pairs={{0,16},{1,17},{2,18},{3,19},{4,20},{5,21},{6,22},{7,23},{8,24},{9,... | collective-permute-start | bytes 884744 | tf_op jit(solution)/shard_map/ppermute | solution.py:396
  6.0 40.2 %collective-permute-start.18 = (bf16[128,1152]{1,0:T(8,128)(2,1)S(1)}, bf16[128,1152]{1,0:T(8,128)(2,1)}, u32[]{:S(2)}, u32[]{:S(2)}) collective-permute-start(bf16[128,1152]{1,0:T(8,128)(2,1)S(1)} %get-tuple-element.161), channel_id=1, source_target_pairs={{0,16},{1,17},{2,18},{3,19},{4,20},{5,21},{6,22},{7,23},{8,24},{9,... | collective-permute-start | bytes 884744 | tf_op jit(solution)/shard_map/ppermute | solution.py:396
  7.5 40.3 %collective-permute-start.1 = (bf16[1728,128]{1,0:T(8,128)(2,1)S(1)}, bf16[1728,128]{1,0:T(8,128)(2,1)S(1)}, u32[]{:S(2)}, u32[]{:S(2)}) collective-permute-start(bf16[1728,128]{1,0:T(8,128)(2,1)S(1)} %constant_dynamic-slice_fusion), channel_id=1, source_target_pairs={{0,2},{1,3},{2,0},{3,1},{4,6},{5,7},{6,4},{7,5},{8,10},{9,11},{10,... | collective-permute-start | bytes 1327112 | tf_op jit(solution)/shard_map/ppermute | solution.py:396
  63.3 38.4 %collective-permute-start.26 = (bf16[128,2304]{1,0:T(8,128)(2,1)S(1)}, bf16[128,2304]{1,0:T(8,128)(2,1)S(1)}, u32[]{:S(2)}, u32[]{:S(2)}) collective-permute-start(bf16[128,2304]{1,0:T(8,128)(2,1)S(1)} %copy-done.3), channel_id=1, source_target_pairs={{0,16},{1,17},{2,18},{3,19},{4,20},{5,21},{6,22},{7,23},{8,24},{9,... | collective-permute-start | bytes 1769480 | tf_op jit(solution)/shard_map/ppermute | solution.py:396
  65.5 42.8 %collective-permute-start.44 = (bf16[128,2304]{1,0:T(8,128)(2,1)S(1)}, bf16[128,2304]{1,0:T(8,128)(2,1)S(1)}, u32[]{:S(2)}, u32[]{:S(2)}) collective-permute-start(bf16[128,2304]{1,0:T(8,128)(2,1)S(1)} %copy-done.1), channel_id=1, source_target_pairs={{0,8},{1,9},{2,10},{3,11},{4,12},{5,13},{6,14},{7,15},{8,0},{9,1},... | collective-permute-start | bytes 1769480 | tf_op jit(solution)/shard_map/ppermute | solution.py:396
  85.8 34.2 %collective-permute-start.54 = (bf16[128,2304]{1,0:T(8,128)(2,1)S(1)}, bf16[128,2304]{1,0:T(8,128)(2,1)S(1)}, u32[]{:S(2)}, u32[]{:S(2)}) collective-permute-start(bf16[128,2304]{1,0:T(8,128)(2,1)S(1)} %copy-done.3), channel_id=1, source_target_pairs={{0,8},{1,9},{2,10},{3,11},{4,12},{5,13},{6,14},{7,15},{8,0},{9,1},... | collective-permute-start | bytes 1769480 | tf_op jit(solution)/shard_map/ppermute | solution.py:396
  101.7 27.9 %collective-permute-start.3 = (bf16[1728,128]{1,0:T(8,128)(2,1)S(1)}, bf16[1728,128]{1,0:T(8,128)(2,1)S(1)}, u32[]{:S(2)}, u32[]{:S(2)}) collective-permute-start(bf16[1728,128]{1,0:T(8,128)(2,1)S(1)} %collective-permute-done.1.refs_5_), channel_id=1, source_target_pairs={{0,8},{1,9},{2,10},{3,11},{4,12},{5,13},{6,14},{7,15},{8,0},{9,1},... | collective-permute-start | bytes 1327112 | tf_op jit(solution)/shard_map/ppermute | solution.py:396
  129.6 23.9 %collective-permute-start.31 = (bf16[72,2304]{1,0:T(8,128)(2,1)}, bf16[72,2304]{1,0:T(8,128)(2,1)S(1)}, u32[]{:S(2)}, u32[]{:S(2)}) collective-permute-start(bf16[72,2304]{1,0:T(8,128)(2,1)} %get-tuple-element.104), channel_id=1, source_target_pairs={{0,5},{1,4},{2,7},{3,6},{4,1},{5,0},{6,3},{7,2},{8,13},{9,12},{10,... | collective-permute-start | bytes 995336 | tf_op jit(solution)/shard_map/ppermute | solution.py:396
  130.1 25.1 %collective-permute-start.32 = (bf16[72,2304]{1,0:T(8,128)(2,1)}, bf16[72,2304]{1,0:T(8,128)(2,1)S(1)}, u32[]{:S(2)}, u32[]{:S(2)}) collective-permute-start(bf16[72,2304]{1,0:T(8,128)(2,1)} %get-tuple-element.105), channel_id=1, source_target_pairs={{0,6},{1,7},{2,4},{3,5},{4,2},{5,3},{6,0},{7,1},{8,14},{9,15},{10,... | collective-permute-start | bytes 995336 | tf_op jit(solution)/shard_map/ppermute | solution.py:396
  136.0 46.5 %collective-permute-start.5 = (bf16[1728,128]{1,0:T(8,128)(2,1)S(1)}, bf16[1728,128]{1,0:T(8,128)(2,1)S(1)}, u32[]{:S(2)}, u32[]{:S(2)}) collective-permute-start(bf16[1728,128]{1,0:T(8,128)(2,1)S(1)} %collective-permute-done.1.refs_5_), channel_id=1, source_target_pairs={{0,1},{1,0},{2,3},{3,2},{4,5},{5,4},{6,7},{7,6},{8,9},{9,8},{10,11... | collective-permute-start | bytes 1327112 | tf_op jit(solution)/shard_map/ppermute | solution.py:396
  136.7 46.5 %collective-permute-start.47 = (bf16[72,2304]{1,0:T(8,128)(2,1)}, bf16[72,2304]{1,0:T(8,128)(2,1)}, u32[]{:S(2)}, u32[]{:S(2)}) collective-permute-start(bf16[72,2304]{1,0:T(8,128)(2,1)} %get-tuple-element.118), channel_id=1, source_target_pairs={{0,1},{1,0},{2,3},{3,2},{4,5},{5,4},{6,7},{7,6},{8,9},{9,8},{10,11... | collective-permute-start | bytes 995336 | tf_op jit(solution)/shard_map/ppermute | solution.py:396
  153.5 30.8 %collective-permute-start.48 = (bf16[72,2304]{1,0:T(8,128)(2,1)}, bf16[72,2304]{1,0:T(8,128)(2,1)}, u32[]{:S(2)}, u32[]{:S(2)}) collective-permute-start(bf16[72,2304]{1,0:T(8,128)(2,1)} %get-tuple-element.119), channel_id=1, source_target_pairs={{0,2},{1,3},{2,0},{3,1},{4,6},{5,7},{6,4},{7,5},{8,10},{9,11},{10,... | collective-permute-start | bytes 995336 | tf_op jit(solution)/shard_map/ppermute | solution.py:396
  155.2 30.9 %collective-permute-start.49 = (bf16[72,2304]{1,0:T(8,128)(2,1)}, bf16[72,2304]{1,0:T(8,128)(2,1)}, u32[]{:S(2)}, u32[]{:S(2)}) collective-permute-start(bf16[72,2304]{1,0:T(8,128)(2,1)} %get-tuple-element.120), channel_id=1, source_target_pairs={{0,3},{1,2},{2,1},{3,0},{4,7},{5,6},{6,5},{7,4},{8,11},{9,10},{10,... | collective-permute-start | bytes 995336 | tf_op jit(solution)/shard_map/ppermute | solution.py:396
  155.3 31.7 %collective-permute-start.55 = (bf16[128,2304]{1,0:T(8,128)(2,1)S(1)}, bf16[128,2304]{1,0:T(8,128)(2,1)}, u32[]{:S(2)}, u32[]{:S(2)}) collective-permute-start(bf16[128,2304]{1,0:T(8,128)(2,1)S(1)} %copy-done.46), channel_id=1, source_target_pairs={{0,8},{1,9},{2,10},{3,11},{4,12},{5,13},{6,14},{7,15},{8,0},{9,1},... | collective-permute-start | bytes 1769480 | tf_op jit(solution)/shard_map/ppermute | solution.py:396
  182.5 25.2 %collective-permute-start.50 = (bf16[72,2304]{1,0:T(8,128)(2,1)}, bf16[72,2304]{1,0:T(8,128)(2,1)S(1)}, u32[]{:S(2)}, u32[]{:S(2)}) collective-permute-start(bf16[72,2304]{1,0:T(8,128)(2,1)} %get-tuple-element.121), channel_id=1, source_target_pairs={{0,4},{1,5},{2,6},{3,7},{4,0},{5,1},{6,2},{7,3},{8,12},{9,13},{10,... | collective-permute-start | bytes 995336 | tf_op jit(solution)/shard_map/ppermute | solution.py:396
  183.3 30.3 %collective-permute-start.51 = (bf16[72,2304]{1,0:T(8,128)(2,1)}, bf16[72,2304]{1,0:T(8,128)(2,1)S(1)}, u32[]{:S(2)}, u32[]{:S(2)}) collective-permute-start(bf16[72,2304]{1,0:T(8,128)(2,1)} %get-tuple-element.122), channel_id=1, source_target_pairs={{0,5},{1,4},{2,7},{3,6},{4,1},{5,0},{6,3},{7,2},{8,13},{9,12},{10,... | collective-permute-start | bytes 995336 | tf_op jit(solution)/shard_map/ppermute | solution.py:396
  184.3 32.1 %collective-permute-start.52 = (bf16[72,2304]{1,0:T(8,128)(2,1)}, bf16[72,2304]{1,0:T(8,128)(2,1)S(1)}, u32[]{:S(2)}, u32[]{:S(2)}) collective-permute-start(bf16[72,2304]{1,0:T(8,128)(2,1)} %get-tuple-element.123), channel_id=1, source_target_pairs={{0,6},{1,7},{2,4},{3,5},{4,2},{5,3},{6,0},{7,1},{8,14},{9,15},{10,... | collective-permute-start | bytes 995336 | tf_op jit(solution)/shard_map/ppermute | solution.py:396
  186.1 31.7 %collective-permute-start.53 = (bf16[72,2304]{1,0:T(8,128)(2,1)}, bf16[72,2304]{1,0:T(8,128)(2,1)S(1)}, u32[]{:S(2)}, u32[]{:S(2)}) collective-permute-start(bf16[72,2304]{1,0:T(8,128)(2,1)} %get-tuple-element.124), channel_id=1, source_target_pairs={{0,7},{1,6},{2,5},{3,4},{4,3},{5,2},{6,1},{7,0},{8,15},{9,14},{10,... | collective-permute-start | bytes 995336 | tf_op jit(solution)/shard_map/ppermute | solution.py:396
  187.0 30.8 %collective-permute-start.34 = (bf16[72,2304]{1,0:T(8,128)(2,1)}, bf16[72,2304]{1,0:T(8,128)(2,1)S(1)}, u32[]{:S(2)}, u32[]{:S(2)}) collective-permute-start(bf16[72,2304]{1,0:T(8,128)(2,1)} %get-tuple-element.108), channel_id=1, source_target_pairs={{0,1},{1,0},{2,3},{3,2},{4,5},{5,4},{6,7},{7,6},{8,9},{9,8},{10,11... | collective-permute-start | bytes 995336 | tf_op jit(solution)/shard_map/ppermute | solution.py:396
  227.0 29.6 %collective-permute-start.60 = (bf16[72,2304]{1,0:T(8,128)(2,1)}, bf16[72,2304]{1,0:T(8,128)(2,1)S(1)}, u32[]{:S(2)}, u32[]{:S(2)}) collective-permute-start(bf16[72,2304]{1,0:T(8,128)(2,1)} %get-tuple-element.130), channel_id=1, source_target_pairs={{0,5},{1,4},{2,7},{3,6},{4,1},{5,0},{6,3},{7,2},{8,13},{9,12},{10,... | collective-permute-start | bytes 995336 | tf_op jit(solution)/shard_map/ppermute | solution.py:396
  227.1 29.8 %collective-permute-start.61 = (bf16[72,2304]{1,0:T(8,128)(2,1)}, bf16[72,2304]{1,0:T(8,128)(2,1)S(1)}, u32[]{:S(2)}, u32[]{:S(2)}) collective-permute-start(bf16[72,2304]{1,0:T(8,128)(2,1)} %get-tuple-element.131), channel_id=1, source_target_pairs={{0,6},{1,7},{2,4},{3,5},{4,2},{5,3},{6,0},{7,1},{8,14},{9,15},{10,... | collective-permute-start | bytes 995336 | tf_op jit(solution)/shard_map/ppermute | solution.py:396
  232.5 27.1 %collective-permute-start.62 = (bf16[72,2304]{1,0:T(8,128)(2,1)}, bf16[72,2304]{1,0:T(8,128)(2,1)S(1)}, u32[]{:S(2)}, u32[]{:S(2)}) collective-permute-start(bf16[72,2304]{1,0:T(8,128)(2,1)} %get-tuple-element.132), channel_id=1, source_target_pairs={{0,7},{1,6},{2,5},{3,4},{4,3},{5,2},{6,1},{7,0},{8,15},{9,14},{10,... | collective-permute-start | bytes 995336 | tf_op jit(solution)/shard_map/ppermute | solution.py:396
  238.9 99.3 %collective-permute-start = (bf16[6912,128]{1,0:T(8,128)(2,1)S(1)}, bf16[6912,128]{1,0:T(8,128)(2,1)S(1)}, u32[]{:S(2)}, u32[]{:S(2)}) collective-permute-start(bf16[6912,128]{1,0:T(8,128)(2,1)S(1)} %constant_dynamic-update-slice_fusion.refs_3_), channel_id=1, source_target_pairs={{0,1},{1,0},{2,3},{3,2},{4,5},{5,4},{6,7},{7,6},{8,9},{9,8},{10,11... | collective-permute-start | bytes 5308424 | tf_op jit(solution)/shard_map/ppermute | solution.py:396
  239.7 49.1 %collective-permute-start.4 = (bf16[1728,128]{1,0:T(8,128)(2,1)}, bf16[1728,128]{1,0:T(8,128)(2,1)S(1)}, u32[]{:S(2)}, u32[]{:S(2)}) collective-permute-start(bf16[1728,128]{1,0:T(8,128)(2,1)} %collective-permute-done.2.refs_6_), channel_id=1, source_target_pairs={{0,8},{1,9},{2,10},{3,11},{4,12},{5,13},{6,14},{7,15},{8,0},{9,1},... | collective-permute-start | bytes 1327112 | tf_op jit(solution)/shard_map/ppermute | solution.py:396
  256.6 30.2 %collective-permute-start.38 = (bf16[72,2304]{1,0:T(8,128)(2,1)}, bf16[72,2304]{1,0:T(8,128)(2,1)}, u32[]{:S(2)}, u32[]{:S(2)}) collective-permute-start(bf16[72,2304]{1,0:T(8,128)(2,1)} %get-tuple-element.112), channel_id=1, source_target_pairs={{0,5},{1,4},{2,7},{3,6},{4,1},{5,0},{6,3},{7,2},{8,13},{9,12},{10,... | collective-permute-start | bytes 995336 | tf_op jit(solution)/shard_map/ppermute | solution.py:396
  256.9 30.2 %collective-permute-start.39 = (bf16[72,2304]{1,0:T(8,128)(2,1)}, bf16[72,2304]{1,0:T(8,128)(2,1)}, u32[]{:S(2)}, u32[]{:S(2)}) collective-permute-start(bf16[72,2304]{1,0:T(8,128)(2,1)} %get-tuple-element.113), channel_id=1, source_target_pairs={{0,6},{1,7},{2,4},{3,5},{4,2},{5,3},{6,0},{7,1},{8,14},{9,15},{10,... | collective-permute-start | bytes 995336 | tf_op jit(solution)/shard_map/ppermute | solution.py:396
  259.6 28.7 %collective-permute-start.40 = (bf16[72,2304]{1,0:T(8,128)(2,1)}, bf16[72,2304]{1,0:T(8,128)(2,1)}, u32[]{:S(2)}, u32[]{:S(2)}) collective-permute-start(bf16[72,2304]{1,0:T(8,128)(2,1)} %get-tuple-element.114), channel_id=1, source_target_pairs={{0,7},{1,6},{2,5},{3,4},{4,3},{5,2},{6,1},{7,0},{8,15},{9,14},{10,... | collective-permute-start | bytes 995336 | tf_op jit(solution)/shard_map/ppermute | solution.py:396
  325.7 36.9 %collective-permute-start.41 = (bf16[128,2304]{1,0:T(8,128)(2,1)}, bf16[128,2304]{1,0:T(8,128)(2,1)S(1)}, u32[]{:S(2)}, u32[]{:S(2)}) collective-permute-start(bf16[128,2304]{1,0:T(8,128)(2,1)} %get-tuple-element.116), channel_id=1, source_target_pairs={{0,16},{1,17},{2,18},{3,19},{4,20},{5,21},{6,22},{7,23},{8,24},{9,... | collective-permute-start | bytes 1769480 | tf_op jit(solution)/shard_map/ppermute | solution.py:396
  335.4 35.0 %collective-permute-start.78 = (bf16[128,1152]{1,0:T(8,128)(2,1)}, bf16[128,1152]{1,0:T(8,128)(2,1)S(1)}, u32[]{:S(2)}, u32[]{:S(2)}) collective-permute-start(bf16[128,1152]{1,0:T(8,128)(2,1)} %get-tuple-element.150), channel_id=1, source_target_pairs={{0,8},{1,9},{2,10},{3,11},{4,12},{5,13},{6,14},{7,15},{8,0},{9,1},... | collective-permute-start | bytes 884744 | tf_op jit(solution)/shard_map/ppermute | solution.py:396
  336.9 33.5 %collective-permute-start.80 = (bf16[128,1152]{1,0:T(8,128)(2,1)}, bf16[128,1152]{1,0:T(8,128)(2,1)S(1)}, u32[]{:S(2)}, u32[]{:S(2)}) collective-permute-start(bf16[128,1152]{1,0:T(8,128)(2,1)} %get-tuple-element.152), channel_id=1, source_target_pairs={{0,24},{1,25},{2,26},{3,27},{4,28},{5,29},{6,30},{7,31},{8,16},{9,... | collective-permute-start | bytes 884744 | tf_op jit(solution)/shard_map/ppermute | solution.py:396
  338.1 38.1 %collective-permute-start.70 = (bf16[128,1152]{1,0:T(8,128)(2,1)}, bf16[128,1152]{1,0:T(8,128)(2,1)S(1)}, u32[]{:S(2)}, u32[]{:S(2)}) collective-permute-start(bf16[128,1152]{1,0:T(8,128)(2,1)} %get-tuple-element.141), channel_id=1, source_target_pairs={{0,8},{1,9},{2,10},{3,11},{4,12},{5,13},{6,14},{7,15},{8,0},{9,1},... | collective-permute-start | bytes 884744 | tf_op jit(solution)/shard_map/ppermute | solution.py:396
  338.2 38.0 %collective-permute-start.79 = (bf16[128,1152]{1,0:T(8,128)(2,1)}, bf16[128,1152]{1,0:T(8,128)(2,1)S(1)}, u32[]{:S(2)}, u32[]{:S(2)}) collective-permute-start(bf16[128,1152]{1,0:T(8,128)(2,1)} %get-tuple-element.151), channel_id=1, source_target_pairs={{0,24},{1,25},{2,26},{3,27},{4,28},{5,29},{6,30},{7,31},{8,16},{9,... | collective-permute-start | bytes 884744 | tf_op jit(solution)/shard_map/ppermute | solution.py:396
  (134 other events, 2772.8 us)
